TPU v7x, 32 devices: a whole 2x2x4 slice. The times are simulated.
32 devices in a mesh: fsdp: 8 (over z, core), tp: 4 (over y, x).
Axes of the slice: x: 2, y: 2, z: 4, core: 2. Of those that a mesh axis runs over, the one named last changes fastest.
Arguments:
- hidden: bfloat16 [3072, 7168], P('fsdp'), may hold values from -72 to 72
- w_query: bfloat16 [7168, 4096], P('fsdp', 'tp'), may hold values from -0.0625 to 0.0625
- w_key: bfloat16 [7168, 1024], P('fsdp', 'tp'), may hold values from -0.0625 to 0.0625
- w_value: bfloat16 [7168, 1024], P('fsdp', 'tp'), may hold values from -0.0625 to 0.0625
- w_out: bfloat16 [4096, 7168], P('tp', 'fsdp'), may hold values from -0.09375 to 0.09375
- exp_query: int32 [56, 32], replicated, may hold values from -1 to 1
- exp_key: int32 [56, 8], replicated, may hold values from -1 to 1
- exp_value: int32 [56, 8], replicated, may hold values from -1 to 1
- exp_out: int32 [32, 56], replicated, may hold values from -1 to 1
- owner: int32 [8], replicated, may hold values from 0 to 7, each once
Outputs:
- attended: bfloat16 [3072, 7168], P('fsdp', 'tp')
Inputs may be any that keep to these rules, and one draw needn't show every extreme that they name: Trainer shard i holds logical slab owner[i]; every slab is held once.
All inputs are finite; a program needn't handle non-finite values.
Results may differ from a plain program's by a relative error of at most 0.038.
Values may be sent and summed in bfloat16 or wider, within the bound.
A program may use at most 128 MiB of HBM per device.

v0:
```python
from functools import partial
import math

import jax
import jax.numpy as jnp
from jax import lax
from jax.experimental import pallas as pl
from jax.experimental.pallas import tpu as pltpu
from jax.sharding import PartitionSpec as P

HQ = 32
HK = 8
HD = 128


neg_large = -1e30


def block_factor(exponents, row_start, row_count, col_start, col_count, block_size):
    repeated = jnp.repeat(exponents, block_size, axis=0)
    picked = lax.dynamic_slice_in_dim(repeated, row_start, row_count, 0)
    repeated = jnp.repeat(picked, block_size, axis=1)
    picked = lax.dynamic_slice_in_dim(repeated, col_start, col_count, 1)
    return jnp.exp2(picked.astype(jnp.float32))


def block_update(state, query_half, pos_half, keys_part, values_part, key_pos, inv_root):
    row_max, row_sum, accum = state
    causal = pos_half[:, None] >= key_pos[None, :]
    scores = (
        jnp.einsum("tgjd,ngd->gjtn", query_half, keys_part, preferred_element_type=jnp.float32)
        * inv_root
    )
    scores = jnp.where(causal, scores, neg_large)
    new_max = jnp.maximum(row_max, jnp.max(scores, axis=3))
    rescale = jnp.exp(row_max - new_max)
    weights = jnp.where(causal, jnp.exp(scores - new_max[..., None]), 0.0)
    row_sum = row_sum * rescale + jnp.sum(weights, axis=3)
    accum = accum * rescale[..., None] + jnp.einsum(
        "gjtn,ngd->gjtd",
        weights.astype(jnp.bfloat16),
        values_part,
        preferred_element_type=jnp.float32,
    )
    return (new_max, row_sum, accum)


def keep_state(state):
    return state


def gather_body(hidden, w_query, w_key, w_value, w_out, exp_query, exp_key, exp_value, exp_out, owner):
    fsdp_index = lax.axis_index("fsdp")
    tp_index = lax.axis_index("tp")
    slab_rows = w_query.shape[0]
    groups = owner.shape[0]
    tokens = hidden.shape[0]
    model_width = hidden.shape[1]
    block_size = model_width // exp_query.shape[0]
    slab_start = owner[fsdp_index] * slab_rows
    query_cols = w_query.shape[1]
    key_cols = w_key.shape[1]

    def scaled_rows(weight, exponents):
        col_count = weight.shape[1]
        factor = block_factor(
            exponents, slab_start, slab_rows, tp_index * col_count, col_count, block_size
        )
        return (weight.astype(jnp.float32) * factor).astype(jnp.bfloat16)

    query_local = scaled_rows(w_query, exp_query)
    key_local = scaled_rows(w_key, exp_key)
    value_local = scaled_rows(w_value, exp_value)
    out_rows = w_out.shape[0]
    out_factor = block_factor(
        exp_out, tp_index * out_rows, out_rows, slab_start, slab_rows, block_size
    )
    out_local = (w_out.astype(jnp.float32) * out_factor).astype(jnp.bfloat16)
    arranged = jnp.take(hidden.reshape(tokens, groups, slab_rows), owner, axis=1).reshape(
        tokens, model_width
    )
    pieces = (
        lax.all_gather(query_local, "fsdp", axis=0, tiled=True),
        lax.all_gather(key_local, "fsdp", axis=0, tiled=True),
        lax.all_gather(value_local, "fsdp", axis=0, tiled=True),
    )
    query_sum, key_sum, value_sum = tuple(
        (jnp.dot(arranged, weight, preferred_element_type=jnp.float32) for weight in pieces)
    )
    query = query_sum.astype(jnp.bfloat16)
    key_here = key_sum.astype(jnp.bfloat16)
    value_here = value_sum.astype(jnp.bfloat16)
    half_rows = tokens // 2
    local_pos = fsdp_index * tokens + jnp.arange(tokens, dtype=jnp.int32)
    group_size = HQ // HK
    kv_heads = key_cols // HD
    query_halves = query.reshape(2, half_rows, kv_heads, group_size, HD)
    pos_halves = local_pos.reshape(2, half_rows)
    pos_top = jnp.max(pos_halves, axis=1)
    inv_root = 1.0 / math.sqrt(HD)
    one_state = (
        jnp.full((kv_heads, group_size, half_rows), neg_large, jnp.float32),
        jnp.zeros((kv_heads, group_size, half_rows), jnp.float32),
        jnp.zeros((kv_heads, group_size, half_rows, HD), jnp.float32),
    )
    offset = jnp.int32(0)
    key_piece = lax.all_gather(key_here, "fsdp", axis=0, tiled=True)
    value_piece = lax.all_gather(value_here, "fsdp", axis=0, tiled=True)
    states = list((one_state, one_state))
    piece_rows = key_piece.shape[0]
    for block_low in range(0, piece_rows, 1024):
        block_high = min(block_low + 1024, piece_rows)
        width_here = block_high - block_low
        keys_part = key_piece[block_low:block_high].reshape(width_here, kv_heads, HD)
        values_part = value_piece[block_low:block_high].reshape(width_here, kv_heads, HD)
        key_pos = offset + block_low + jnp.arange(width_here, dtype=jnp.int32)
        for attend_which in range(2):
            update = partial(
                block_update,
                query_half=query_halves[attend_which],
                pos_half=pos_halves[attend_which],
                keys_part=keys_part,
                values_part=values_part,
                key_pos=key_pos,
                inv_root=inv_root,
            )
            states[attend_which] = lax.cond(
                offset + block_low <= pos_top[attend_which],
                update,
                keep_state,
                states[attend_which],
            )
    final_states = tuple(states)
    context_parts = []
    for which in range(2):
        row_max, row_sum, accum = final_states[which]
        part_context = (accum / row_sum[..., None]).astype(jnp.bfloat16)
        context_parts.append(part_context.transpose(2, 0, 1, 3).reshape(half_rows, query_cols))
    context = jnp.concatenate(context_parts, axis=0)
    column_terms = jnp.dot(
        context,
        lax.all_gather(out_local, "fsdp", axis=1, tiled=True),
        preferred_element_type=jnp.float32,
    )
    slab_ids = jnp.arange(groups, dtype=jnp.int32)
    inverse = jnp.sum(
        slab_ids[:, None] * (owner[:, None] == slab_ids[None, :]).astype(jnp.int32), axis=0
    )
    ordered = jnp.take(column_terms.reshape(tokens, groups, slab_rows), inverse, axis=1).reshape(
        tokens, model_width
    )
    result = lax.psum_scatter(ordered.astype(jnp.bfloat16), "tp", scatter_dimension=1, tiled=True)
    return result


MESH = pl.DeviceIdType.MESH
VMEM = pltpu.VMEM


def greet(peers):
    barrier = pltpu.get_barrier_semaphore()
    for device in peers:
        pl.semaphore_signal(barrier, inc=1, device_id=device, device_id_type=MESH)
    pl.semaphore_wait(barrier, len(peers))


def near_first(n):
    steps = []
    for d in range(1, n // 2 + 1):
        steps.append(d)
        if n - d != d:
            steps.append(n - d)
    return steps


def spread_kernel(n_f, n_t, piece_ref, out_ref, send_one, send_two, recv, local_sem):
    f = lax.axis_index("fsdp")
    t = lax.axis_index("tp")
    far = [lax.rem(f + d, n_f) for d in range(n_f)]
    side = [lax.rem(t + k, n_t) for k in range(n_t)]
    greet([{"fsdp": far[d]} for d in range(1, n_f)] + [{"tp": side[k]} for k in range(1, n_t)])
    own = pltpu.make_async_copy(piece_ref.at[f], out_ref.at[f, t], local_sem)
    own.start()
    copies = []
    order = near_first(n_f)
    for d in order:
        copies.append(
            pltpu.make_async_remote_copy(
                src_ref=piece_ref.at[far[d]],
                dst_ref=out_ref.at[f, t],
                send_sem=send_one.at[d],
                recv_sem=recv.at[f, t],
                device_id={"fsdp": far[d]},
                device_id_type=MESH,
            )
        )
        copies[-1].start()

    def forward(slot, source, from_f):
        for k in range(1, n_t):
            copies.append(
                pltpu.make_async_remote_copy(
                    src_ref=source,
                    dst_ref=out_ref.at[from_f, t],
                    send_sem=send_two.at[slot, k],
                    recv_sem=recv.at[from_f, t],
                    device_id={"tp": side[k]},
                    device_id_type=MESH,
                )
            )
            copies[-1].start()

    def arrived(from_f, from_t):
        pltpu.make_async_remote_copy(
            src_ref=piece_ref.at[0],
            dst_ref=out_ref.at[from_f, from_t],
            send_sem=send_one.at[0],
            recv_sem=recv.at[from_f, from_t],
            device_id={"tp": side[1]},
            device_id_type=MESH,
        ).wait_recv()

    forward(0, piece_ref.at[f], f)
    for d in order:
        source = lax.rem(f - d + n_f, n_f)
        arrived(source, t)
        forward(d, out_ref.at[source, t], source)
    for d in [0] + order:
        for k in range(1, n_t):
            arrived(lax.rem(f - d + n_f, n_f), lax.rem(t - k + n_t, n_t))
    for copy in copies:
        copy.wait_send()
    own.wait()


def spread(pieces, n_f, n_t):
    _, rows, cols = pieces.shape
    return pl.pallas_call(
        partial(spread_kernel, n_f, n_t),
        out_shape=jax.ShapeDtypeStruct((n_f, n_t, rows, cols), pieces.dtype),
        in_specs=[pl.BlockSpec(memory_space=VMEM)],
        out_specs=pl.BlockSpec(memory_space=VMEM),
        scratch_shapes=[
            pltpu.SemaphoreType.DMA((n_f,)),
            pltpu.SemaphoreType.DMA((n_f, n_t)),
            pltpu.SemaphoreType.DMA((n_f, n_t)),
            pltpu.SemaphoreType.DMA,
        ],
        compiler_params=pltpu.CompilerParams(collective_id=0, has_side_effects=True),
        name="spread_hidden",
    )(pieces)


def exchange_kernel(n, axis, piece_ref, out_ref, send, recv, local_sem):
    me = lax.axis_index(axis)
    peers = [lax.rem(me + d, n) for d in range(n)]
    greet([{axis: peers[d]} for d in range(1, n)])
    own = pltpu.make_async_copy(piece_ref.at[me], out_ref.at[me], local_sem)
    own.start()
    copies = []
    for d in near_first(n):
        copies.append(
            pltpu.make_async_remote_copy(
                src_ref=piece_ref.at[peers[d]],
                dst_ref=out_ref.at[me],
                send_sem=send.at[d],
                recv_sem=recv.at[me],
                device_id={axis: peers[d]},
                device_id_type=MESH,
            )
        )
        copies[-1].start()
    for d in near_first(n):
        source = lax.rem(me - d + n, n)
        pltpu.make_async_remote_copy(
            src_ref=piece_ref.at[0],
            dst_ref=out_ref.at[source],
            send_sem=send.at[0],
            recv_sem=recv.at[source],
            device_id={axis: peers[1]},
            device_id_type=MESH,
        ).wait_recv()
    for copy in copies:
        copy.wait_send()
    own.wait()


def exchange(pieces, n, axis, collective_id):
    return pl.pallas_call(
        partial(exchange_kernel, n, axis),
        out_shape=jax.ShapeDtypeStruct(pieces.shape, pieces.dtype),
        in_specs=[pl.BlockSpec(memory_space=VMEM)],
        out_specs=pl.BlockSpec(memory_space=VMEM),
        scratch_shapes=[
            pltpu.SemaphoreType.DMA((n,)),
            pltpu.SemaphoreType.DMA((n,)),
            pltpu.SemaphoreType.DMA,
        ],
        compiler_params=pltpu.CompilerParams(collective_id=collective_id, has_side_effects=True),
        name="exchange_" + axis,
    )(pieces)


def scale_into(out_ref, w_ref, fac_ref, at, blocks, block):
    for b in range(blocks):
        rows = slice(b * block, (b + 1) * block)
        for c in range(0, w_ref.shape[1], block):
            cols = slice(at + c, at + c + block)
            weight = w_ref[rows, c : c + block].astype(jnp.float32)
            out_ref[rows, cols] = (weight * fac_ref[b : b + 1, cols]).astype(jnp.bfloat16)


def project_kernel(heads, kv_heads, share, block, h_ref, wq_ref, wk_ref, wv_ref, fac_ref, out_ref, w_scr):
    q_cols = wq_ref.shape[1]
    k_cols = wk_ref.shape[1]
    blocks = wq_ref.shape[0] // block

    @pl.when(pl.program_id(0) == 0)
    def _():
        scale_into(w_scr, wq_ref, fac_ref, 0, blocks, block)
        scale_into(w_scr, wk_ref, fac_ref, q_cols, blocks, block)
        scale_into(w_scr, wv_ref, fac_ref, q_cols + k_cols, blocks, block)

    rows = h_ref.shape[0]
    part = rows // share
    both = jnp.dot(h_ref[...], w_scr[:, :], preferred_element_type=jnp.float32).astype(jnp.bfloat16)
    for j in range(heads):
        g, p = j // share, j % share
        out_ref[j, 0, :rows, :] = both[:, j * HD : (j + 1) * HD]
        span = slice(p * part, (p + 1) * part)
        k_at = q_cols + g * HD
        v_at = q_cols + k_cols + g * HD
        out_ref[j, 0, rows : rows + part, :] = both[span, k_at : k_at + HD]
        out_ref[j, 0, rows + part :, :] = both[span, v_at : v_at + HD]


def attend_kernel(inv_root, key_rows, q_ref, k_ref, v_ref, out_ref):
    i = pl.program_id(0)
    rows = q_ref.shape[0]
    query = q_ref[...]

    def step(j, state, masked):
        row_max, row_sum, accum = state
        at = pl.ds(pl.multiple_of(j * key_rows, key_rows), key_rows)
        scores = (
            lax.dot_general(
                query, k_ref[at, :], (((1,), (1,)), ((), ())), preferred_element_type=jnp.float32
            )
            * inv_root
        )
        if masked:
            q_pos = lax.broadcasted_iota(jnp.int32, scores.shape, 0)
            k_pos = lax.broadcasted_iota(jnp.int32, scores.shape, 1)
            scores = jnp.where(q_pos >= k_pos, scores, neg_large)
        new_max = jnp.maximum(row_max, jnp.max(scores, axis=1, keepdims=True))
        rescale = jnp.exp(row_max - new_max)
        weights = jnp.exp(scores - new_max)
        row_sum = row_sum * rescale + jnp.sum(weights, axis=1, keepdims=True)
        accum = accum * rescale + jnp.dot(
            weights.astype(jnp.bfloat16), v_ref[at, :], preferred_element_type=jnp.float32
        )
        return (new_max, row_sum, accum)

    state = (
        jnp.full((rows, 1), neg_large, jnp.float32),
        jnp.zeros((rows, 1), jnp.float32),
        jnp.zeros((rows, HD), jnp.float32),
    )
    state = step(i, state, True)
    _, row_sum, accum = lax.fori_loop(0, i, lambda j, s: step(j, s, False), state)
    out_ref[...] = (accum / row_sum).astype(jnp.bfloat16)


def out_kernel(heads, block, n_t, c_ref, w_ref, fac_ref, out_ref, w_scr):
    blocks = w_ref.shape[0] // block

    @pl.when(pl.program_id(0) == 0)
    def _():
        w_scr[...] = jnp.zeros_like(w_scr)
        scale_into(w_scr, w_ref, fac_ref, 0, blocks, block)

    context = jnp.concatenate([c_ref[h] for h in range(heads)], axis=1)
    part = jnp.dot(context, w_scr[...], preferred_element_type=jnp.float32).astype(jnp.bfloat16)
    quarter, slab = out_ref.shape[2], out_ref.shape[3]
    for r in range(n_t):
        out_ref[r, 0, :, :] = part[r * quarter : (r + 1) * quarter, :slab]


def stationary_body(
    n_f, n_t, hidden, w_query, w_key, w_value, w_out, exp_query, exp_key, exp_value, exp_out, owner
):
    f = lax.axis_index("fsdp")
    t = lax.axis_index("tp")
    here, width = hidden.shape
    slab = w_query.shape[0]
    tokens = here * n_f
    block = width // exp_query.shape[0]
    slab_blocks = slab // block
    q_cols, k_cols = w_query.shape[1], w_key.shape[1]
    heads, kv_heads = q_cols // HD, k_cols // HD
    share = heads // kv_heads
    quarter = here // n_t
    logical = owner[f]

    def factors(exponents, cols):
        picked = lax.dynamic_slice(
            exponents, (logical * slab_blocks, t * (cols // block)), (slab_blocks, cols // block)
        )
        return jnp.repeat(jnp.exp2(picked.astype(jnp.float32)), block, axis=1)

    in_factor = jnp.concatenate(
        [factors(exp_query, q_cols), factors(exp_key, k_cols), factors(exp_value, k_cols)], axis=1
    )
    out_rows = w_out.shape[0] // block
    out_factor = jnp.repeat(
        jnp.exp2(
            lax.dynamic_slice(
                exp_out, (t * out_rows, logical * slab_blocks), (out_rows, slab_blocks)
            ).astype(jnp.float32)
        ),
        block,
        axis=1,
    )

    in_factor = jnp.pad(in_factor, ((0, -slab_blocks % 8), (0, 0)))
    out_factor = jnp.pad(out_factor, ((0, -out_rows % 8), (0, -slab % 256)))

    mine = lax.dynamic_slice_in_dim(hidden, t * quarter, quarter, 0)
    pieces = jnp.stack(
        [lax.dynamic_slice_in_dim(mine, owner[i] * slab, slab, 1) for i in range(n_f)]
    )
    arranged = spread(pieces, n_f, n_t).reshape(tokens, slab)

    steps = share
    rows = tokens // steps
    part = rows // share
    whole = lambda a: pl.BlockSpec(a.shape, lambda i: (0,) * a.ndim)
    packed = pl.pallas_call(
        partial(project_kernel, heads, kv_heads, share, block),
        grid=(steps,),
        out_shape=jax.ShapeDtypeStruct((heads, steps, rows + 2 * part, HD), jnp.bfloat16),
        in_specs=[
            pl.BlockSpec((rows, slab), lambda i: (i, 0)),
            whole(w_query),
            whole(w_key),
            whole(w_value),
            whole(in_factor),
        ],
        out_specs=pl.BlockSpec((heads, 1, rows + 2 * part, HD), lambda i: (0, i, 0, 0)),
        scratch_shapes=[pltpu.VMEM((slab, q_cols + 2 * k_cols), jnp.bfloat16)],
        compiler_params=pltpu.CompilerParams(vmem_limit_bytes=56 * 1024 * 1024),
        name="project",
    )(arranged, w_query, w_key, w_value, in_factor)
    summed = lax.psum_scatter(packed, "fsdp", scatter_dimension=0, tiled=False)

    groups = [[g * share + p for p in range(share)] for g in range(kv_heads)]
    kv = lax.all_gather(
        summed[:, rows:, :].reshape(steps, 2, part, HD),
        "fsdp",
        axis=1,
        tiled=False,
        axis_index_groups=groups,
    )
    kv = kv.transpose(2, 0, 1, 3, 4).reshape(2, tokens, HD)
    query = summed[:, :rows, :].reshape(tokens, HD)
    tile = here
    context = pl.pallas_call(
        partial(attend_kernel, 1.0 / math.sqrt(HD), tile),
        grid=(tokens // tile,),
        out_shape=jax.ShapeDtypeStruct((tokens, HD), jnp.bfloat16),
        in_specs=[
            pl.BlockSpec((tile, HD), lambda i: (i, 0)),
            pl.BlockSpec((pl.squeezed, tokens, HD), lambda i: (0, 0, 0)),
            pl.BlockSpec((pl.squeezed, tokens, HD), lambda i: (1, 0, 0)),
        ],
        out_specs=pl.BlockSpec((tile, HD), lambda i: (i, 0)),
        compiler_params=pltpu.CompilerParams(vmem_limit_bytes=48 * 1024 * 1024),
        name="attend",
    )(query, kv, kv)

    gathered = lax.all_gather(context, "fsdp", axis=0, tiled=False)
    parts = pl.pallas_call(
        partial(out_kernel, heads, block, n_t),
        grid=(n_f,),
        out_shape=jax.ShapeDtypeStruct((n_t, n_f, quarter, slab), jnp.bfloat16),
        in_specs=[
            pl.BlockSpec((heads, here, HD), lambda i: (0, i, 0)),
            whole(w_out),
            whole(out_factor),
        ],
        out_specs=pl.BlockSpec((n_t, 1, quarter, slab), lambda i: (0, i, 0, 0)),
        scratch_shapes=[pltpu.VMEM((w_out.shape[0], slab + -slab % 256), jnp.bfloat16)],
        compiler_params=pltpu.CompilerParams(vmem_limit_bytes=48 * 1024 * 1024),
        name="project_out",
    )(gathered, w_out, out_factor)
    total = lax.psum_scatter(parts, "tp", scatter_dimension=0, tiled=False)

    by_slab = exchange(total, n_f, "fsdp", 1)
    slab_ids = jnp.arange(n_f, dtype=jnp.int32)
    inverse = jnp.sum(
        slab_ids[:, None] * (owner[:, None] == slab_ids[None, :]).astype(jnp.int32), axis=0
    )
    per = n_f // n_t
    columns = jnp.stack(
        [
            jnp.concatenate([by_slab[inverse[r * per + c]] for c in range(per)], axis=1)
            for r in range(n_t)
        ]
    )
    return exchange(columns, n_t, "tp", 2).reshape(here, width // n_t)


def solution(mesh):
    n_f, n_t = mesh.shape["fsdp"], mesh.shape["tp"]

    def body(*arrays):
        hidden, w_query, w_key = arrays[0], arrays[1], arrays[2]
        heads, kv_heads = w_query.shape[1] // HD, w_key.shape[1] // HD
        fits = heads == n_f and n_f % n_t == 0 and hidden.shape[0] % (16 * n_t) == 0
        if fits:
            return stationary_body(n_f, n_t, *arrays)
        return gather_body(*arrays)

    placed = (
        P("fsdp", None),
        P("fsdp", "tp"),
        P("fsdp", "tp"),
        P("fsdp", "tp"),
        P("tp", "fsdp"),
        P(),
        P(),
        P(),
        P(),
        P(),
    )
    return jax.shard_map(
        body, mesh=mesh, in_specs=placed, out_specs=P("fsdp", "tp"), check_vma=False
    )
```

profile of v0, /device:TPU:25, one launch (start us, length us, event | category | flops | bytes accessed | tf_op | source)
XLA Modules:
  0.0 461.9 jit_solution(13685600665894538457)
XLA Ops:
  6.5 1.7 fusion.1
  13.2 1.1 bitcast_dynamic-update-slice_fusion.7
  14.3 1.1 bitcast_dynamic-update-slice_fusion.6
  15.4 1.1 bitcast_dynamic-update-slice_fusion.5
  16.5 1.1 bitcast_dynamic-update-slice_fusion.4
  17.5 1.1 bitcast_dynamic-update-slice_fusion.3
  18.6 1.1 bitcast_dynamic-update-slice_fusion.2
  19.7 1.1 bitcast_dynamic-update-slice_fusion.1
  20.8 1.1 bitcast_dynamic-update-slice_fusion.piece_ref
  21.9 1.1 copy-done.2
  22.9 66.8 %spread_hidden.1 = bf16[8,4,96,896]{3,2,1,0:T(8,128)(2,1)} custom-call(bf16[8,96,896]{2,1,0:T(8,128)(2,1)} %copy-done.2), custom_call_target="tpu_custom_call" | custom-call | tf_op jit(solution)/shard_map/spread_hidden/pallas_call | solution.py:238
  90.4 0.8 multiply_exponential_fusion.1
  91.2 0.1 copy.21
  91.3 0.1 broadcast_bitcast_fusion.1
  91.4 0.8 multiply_exponential_fusion.2
  92.2 0.1 copy.23
  92.3 0.1 broadcast_bitcast_fusion.2
  92.4 0.1 copy.22
  92.5 0.1 broadcast_bitcast_fusion.3
  92.5 0.6 select_maximum_fusion.fac_ref
  93.2 14.6 %project.1 = bf16[8,4,1152,128]{3,2,1,0:T(8,128)(2,1)} custom-call(bf16[3072,896]{1,0:T(8,128)(2,1)} %bitcast.88, bf16[896,1024]{1,0:T(8,128)(2,1)} %wq_ref.1, bf16[896,256]{1,0:T(8,128)(2,1)} %wk_ref.1, bf16[896,256]{1,0:T(8,128)(2,1)} %wv_ref.1, f32[8,1536]{1,0:T(8,128)} %select_maximum_fusion.fac_ref), custom_call_target="tpu_custom_call" | custom-call | tf_op jit(solution)/shard_map/project/pallas_call | solution.py:438
  107.8 0.0 reduce-scatter.5.cloned.1.call-update
  107.8 0.0 all-gather.4.cloned.1.call-start
  107.8 98.3 %reduce-scatter.5.cloned.1.call-done = bf16[1,4,1152,128]{3,2,1,0:T(8,128)(2,1)} async-done(((bf16[8,4,1152,128]{3,2,1,0:T(8,128)(2,1)}), bf16[1,4,1152,128]{3,2,1,0:T(8,128)(2,1)}) %reduce-scatter.5.cloned.1.call-update) | async-done | bytes 1179664 | tf_op jit(solution)/shard_map/reduce_scatter | solution.py:454
  206.1 1.1 slice.73
  207.2 0.8 copy.24
  208.0 0.0 all-gather.4.cloned.1.call-update
  208.0 0.0 all-gather.6.cloned.1.call-start
  208.1 0.1 slice.72
  208.1 23.0 %all-gather.4.cloned.1.call-done = bf16[4,4,2,192,128]{4,3,1,0,2:T(8,128)(2,1)} async-done(((bf16[4,1,2,192,128]{4,3,1,0,2:T(8,128)(2,1)}), bf16[4,4,2,192,128]{4,3,1,0,2:T(8,128)(2,1)}) %all-gather.4.cloned.1.call-update) | async-done | bytes 1572880 | tf_op jit(solution)/shard_map/all_gather | solution.py:457
  231.1 1.4 copy-done
  232.5 21.1 %attend.1 = bf16[3072,128]{1,0:T(8,128)(2,1)} custom-call(bf16[3072,128]{1,0:T(8,128)(2,1)S(1)} %bitcast.87, bf16[2,3072,128]{2,1,0:T(8,128)(2,1)S(1)} %bitcast.85, bf16[2,3072,128]{2,1,0:T(8,128)(2,1)S(1)} %bitcast.86), custom_call_target="tpu_custom_call" | custom-call | tf_op jit(solution)/shard_map/attend/pallas_call | solution.py:467
  253.6 0.0 all-gather.6.cloned.1.call-update
  253.6 0.0 reduce-scatter.7.cloned.1.call-start
  253.7 0.8 multiply_exponential_fusion
  254.4 0.1 copy.25
  254.5 0.1 broadcast_bitcast_fusion
  254.6 62.1 %all-gather.6.cloned.1.call-done = bf16[24576,128]{1,0:T(8,128)(2,1)} async-done(((bf16[3072,128]{1,0:T(8,128)(2,1)}), bf16[24576,128]{1,0:T(8,128)(2,1)}) %all-gather.6.cloned.1.call-update) | async-done | bytes 6291472 | tf_op jit(solution)/shard_map/all_gather | solution.py:481
  316.7 11.9 %project_out.1 = bf16[4,8,96,896]{3,2,1,0:T(8,128)(2,1)} custom-call(bf16[8,3072,128]{2,1,0:T(8,128)(2,1)} %bitcast.89, bf16[1024,896]{1,0:T(8,128)(2,1)S(1)} %copy-done.1, f32[8,1024]{1,0:T(8,128)S(1)} %pad.9.fac_ref), custom_call_target="tpu_custom_call" | custom-call | tf_op jit(solution)/shard_map/project_out/pallas_call | solution.py:482
  328.6 0.6 copy-done.4
  329.3 0.1 select_reduce_fusion
  329.4 0.7 fusion
  345.1 47.8 %reduce-scatter.7.cloned.1.call-done = bf16[1,8,96,896]{3,2,1,0:T(8,128)(2,1)} async-done(((bf16[4,8,96,896]{3,2,1,0:T(8,128)(2,1)}), bf16[1,8,96,896]{3,2,1,0:T(8,128)(2,1)}) %reduce-scatter.7.cloned.1.call-update) | async-done | bytes 1376272
  393.0 36.0 %exchange_fsdp.1 = bf16[8,96,896]{2,1,0:T(8,128)(2,1)} custom-call(bf16[8,96,896]{2,1,0:T(8,128)(2,1)} %bitcast.92), custom_call_target="tpu_custom_call" | custom-call | tf_op jit(solution)/shard_map/exchange_fsdp/pallas_call | solution.py:289
  429.0 1.5 dynamic-slice_bitcast_fusion.7
  430.7 1.3 pad_maximum_fusion.piece_ref
  431.9 20.9 %exchange_tp.1 = bf16[4,96,1792]{2,1,0:T(8,128)(2,1)} custom-call(bf16[4,96,1792]{2,1,0:T(8,128)(2,1)} %pad_maximum_fusion.piece_ref), custom_call_target="tpu_custom_call" | custom-call | tf_op jit(solution)/shard_map/exchange_tp/pallas_call | solution.py:289
  452.8 2.5 copy.43
  (17 shorter events, 0.2 us)
Async XLA Ops:
  6.5 199.6 %reduce-scatter.5.cloned.1.call-start = ((), (), s32[]{:S(2)}) async-start(), calls=%async_computation.2 | async-start | bytes 10616832 | tf_op jit(solution)/shard_map/reduce_scatter | solution.py:454
  21.9 1.1 copy-start.2
  107.8 123.3 %all-gather.4.cloned.1.call-start = ((), (), s32[]{:S(2)}) async-start(), calls=%async_computation.3 | async-start | bytes 1966080 | tf_op jit(solution)/shard_map/all_gather | solution.py:457
  206.1 2.0 copy-start.3
  208.0 108.7 %all-gather.6.cloned.1.call-start = ((), (), s32[]{:S(2)}) async-start(), calls=%async_computation.4 | async-start | bytes 7077888 | tf_op jit(solution)/shard_map/all_gather | solution.py:481
  231.1 1.4 copy-start
  232.5 84.2 %copy-start.1 = (bf16[1024,896]{1,0:T(8,128)(2,1)S(1)}, bf16[1024,896]{1,0:T(8,128)(2,1)}, u32[]{:S(2)}) copy-start(bf16[1024,896]{1,0:T(8,128)(2,1)} %w_ref.1) | copy-start | bytes 5505028
  253.6 139.3 %reduce-scatter.7.cloned.1.call-start = ((), (), s32[]{:S(2)}) async-start(), calls=%async_computation.5 | async-start | bytes 6881280
  328.6 0.7 copy-start.4
Sparse Core Ops, SparseCore 0:
  107.9 98.1 reduce-scatter.4
  208.1 22.9 all-gather.3
  253.7 62.9 all-gather.5
  328.8 64.1 reduce-scatter.6
where the time goes:
time: 466 us; the launch traced here: 462 us
  waiting for transfers between devices  231 us (50%)
  Pallas kernels  171 us (37%)
  between operations  34 us (7%)
  local copies, waits for them, and re-layouts  20.8 us (4%)
    reduce_scatter x1, waiting for transfers between devices, stationary_body(): summed = lax.psum_scatter(packed, 'fsdp', scatter_dimension=0, tiled=False)  98.3 us
    pallas_call x1, Pallas kernels, spread(): pl.pallas_call(partial(spread_kernel, n_f, n_t), out_shape=jax.ShapeDtype...  66.8 us
    all_gather x1, waiting for transfers between devices, stationary_body(): gathered = lax.all_gather(context, 'fsdp', axis=0, tiled=False)  62.1 us
    pallas_call x2, Pallas kernels, exchange(): pl.pallas_call(partial(exchange_kernel, n, axis), out_shape=jax.ShapeDtyp...  56.9 us
    unnamed x5, waiting for transfers between devices  47.9 us
    all_gather x1, waiting for transfers between devices, stationary_body(): lax.all_gather(summed[:, rows:, :].reshape(steps, 2, part, HD), 'fsdp', a...  23 us
    pallas_call x1, Pallas kernels, stationary_body(): pl.pallas_call(partial(attend_kernel, 1.0 / math.sqrt(HD), tile), grid=(t...  21.1 us
    pallas_call x1, Pallas kernels, stationary_body(): pl.pallas_call(partial(project_kernel, heads, kv_heads, share, block), gr...  14.6 us
  transfers between devices with their start and end apart: 4, of which 4 were waited for; matrix products, arithmetic and copies ran while one was open for 0% of the time, Pallas kernels for 0%

commit v1 on v0

v1 whole, which is shorter than its diff:
```python
from functools import partial
import math

import jax
import jax.numpy as jnp
from jax import lax
from jax.experimental import pallas as pl
from jax.experimental.pallas import tpu as pltpu
from jax.sharding import PartitionSpec as P

HQ = 32
HK = 8
HD = 128


neg_large = -1e30


def block_factor(exponents, row_start, row_count, col_start, col_count, block_size):
    repeated = jnp.repeat(exponents, block_size, axis=0)
    picked = lax.dynamic_slice_in_dim(repeated, row_start, row_count, 0)
    repeated = jnp.repeat(picked, block_size, axis=1)
    picked = lax.dynamic_slice_in_dim(repeated, col_start, col_count, 1)
    return jnp.exp2(picked.astype(jnp.float32))


def block_update(state, query_half, pos_half, keys_part, values_part, key_pos, inv_root):
    row_max, row_sum, accum = state
    causal = pos_half[:, None] >= key_pos[None, :]
    scores = (
        jnp.einsum("tgjd,ngd->gjtn", query_half, keys_part, preferred_element_type=jnp.float32)
        * inv_root
    )
    scores = jnp.where(causal, scores, neg_large)
    new_max = jnp.maximum(row_max, jnp.max(scores, axis=3))
    rescale = jnp.exp(row_max - new_max)
    weights = jnp.where(causal, jnp.exp(scores - new_max[..., None]), 0.0)
    row_sum = row_sum * rescale + jnp.sum(weights, axis=3)
    accum = accum * rescale[..., None] + jnp.einsum(
        "gjtn,ngd->gjtd",
        weights.astype(jnp.bfloat16),
        values_part,
        preferred_element_type=jnp.float32,
    )
    return (new_max, row_sum, accum)


def keep_state(state):
    return state


def gather_body(hidden, w_query, w_key, w_value, w_out, exp_query, exp_key, exp_value, exp_out, owner):
    fsdp_index = lax.axis_index("fsdp")
    tp_index = lax.axis_index("tp")
    slab_rows = w_query.shape[0]
    groups = owner.shape[0]
    tokens = hidden.shape[0]
    model_width = hidden.shape[1]
    block_size = model_width // exp_query.shape[0]
    slab_start = owner[fsdp_index] * slab_rows
    query_cols = w_query.shape[1]
    key_cols = w_key.shape[1]

    def scaled_rows(weight, exponents):
        col_count = weight.shape[1]
        factor = block_factor(
            exponents, slab_start, slab_rows, tp_index * col_count, col_count, block_size
        )
        return (weight.astype(jnp.float32) * factor).astype(jnp.bfloat16)

    query_local = scaled_rows(w_query, exp_query)
    key_local = scaled_rows(w_key, exp_key)
    value_local = scaled_rows(w_value, exp_value)
    out_rows = w_out.shape[0]
    out_factor = block_factor(
        exp_out, tp_index * out_rows, out_rows, slab_start, slab_rows, block_size
    )
    out_local = (w_out.astype(jnp.float32) * out_factor).astype(jnp.bfloat16)
    arranged = jnp.take(hidden.reshape(tokens, groups, slab_rows), owner, axis=1).reshape(
        tokens, model_width
    )
    pieces = (
        lax.all_gather(query_local, "fsdp", axis=0, tiled=True),
        lax.all_gather(key_local, "fsdp", axis=0, tiled=True),
        lax.all_gather(value_local, "fsdp", axis=0, tiled=True),
    )
    query_sum, key_sum, value_sum = tuple(
        (jnp.dot(arranged, weight, preferred_element_type=jnp.float32) for weight in pieces)
    )
    query = query_sum.astype(jnp.bfloat16)
    key_here = key_sum.astype(jnp.bfloat16)
    value_here = value_sum.astype(jnp.bfloat16)
    half_rows = tokens // 2
    local_pos = fsdp_index * tokens + jnp.arange(tokens, dtype=jnp.int32)
    group_size = HQ // HK
    kv_heads = key_cols // HD
    query_halves = query.reshape(2, half_rows, kv_heads, group_size, HD)
    pos_halves = local_pos.reshape(2, half_rows)
    pos_top = jnp.max(pos_halves, axis=1)
    inv_root = 1.0 / math.sqrt(HD)
    one_state = (
        jnp.full((kv_heads, group_size, half_rows), neg_large, jnp.float32),
        jnp.zeros((kv_heads, group_size, half_rows), jnp.float32),
        jnp.zeros((kv_heads, group_size, half_rows, HD), jnp.float32),
    )
    offset = jnp.int32(0)
    key_piece = lax.all_gather(key_here, "fsdp", axis=0, tiled=True)
    value_piece = lax.all_gather(value_here, "fsdp", axis=0, tiled=True)
    states = list((one_state, one_state))
    piece_rows = key_piece.shape[0]
    for block_low in range(0, piece_rows, 1024):
        block_high = min(block_low + 1024, piece_rows)
        width_here = block_high - block_low
        keys_part = key_piece[block_low:block_high].reshape(width_here, kv_heads, HD)
        values_part = value_piece[block_low:block_high].reshape(width_here, kv_heads, HD)
        key_pos = offset + block_low + jnp.arange(width_here, dtype=jnp.int32)
        for attend_which in range(2):
            update = partial(
                block_update,
                query_half=query_halves[attend_which],
                pos_half=pos_halves[attend_which],
                keys_part=keys_part,
                values_part=values_part,
                key_pos=key_pos,
                inv_root=inv_root,
            )
            states[attend_which] = lax.cond(
                offset + block_low <= pos_top[attend_which],
                update,
                keep_state,
                states[attend_which],
            )
    final_states = tuple(states)
    context_parts = []
    for which in range(2):
        row_max, row_sum, accum = final_states[which]
        part_context = (accum / row_sum[..., None]).astype(jnp.bfloat16)
        context_parts.append(part_context.transpose(2, 0, 1, 3).reshape(half_rows, query_cols))
    context = jnp.concatenate(context_parts, axis=0)
    column_terms = jnp.dot(
        context,
        lax.all_gather(out_local, "fsdp", axis=1, tiled=True),
        preferred_element_type=jnp.float32,
    )
    slab_ids = jnp.arange(groups, dtype=jnp.int32)
    inverse = jnp.sum(
        slab_ids[:, None] * (owner[:, None] == slab_ids[None, :]).astype(jnp.int32), axis=0
    )
    ordered = jnp.take(column_terms.reshape(tokens, groups, slab_rows), inverse, axis=1).reshape(
        tokens, model_width
    )
    result = lax.psum_scatter(ordered.astype(jnp.bfloat16), "tp", scatter_dimension=1, tiled=True)
    return result


MESH = pl.DeviceIdType.MESH
VMEM = pltpu.VMEM
SMEM = pltpu.SMEM
DMA = pltpu.SemaphoreType.DMA
CORES = 2


def greet(peers):
    barrier = pltpu.get_barrier_semaphore()
    for device in peers:
        pl.semaphore_signal(barrier, inc=1, device_id=device, device_id_type=MESH)
    pl.semaphore_wait(barrier, len(peers))


def greet_all(n_f, n_t, f, t):
    greet(
        [{"fsdp": lax.rem(f + d, n_f)} for d in range(1, n_f)]
        + [{"tp": lax.rem(t + k, n_t)} for k in range(1, n_t)]
    )


def remote(src, dst, send, recv, device):
    return pltpu.make_async_remote_copy(
        src_ref=src,
        dst_ref=dst,
        send_sem=send,
        recv_sem=recv,
        device_id=device,
        device_id_type=MESH,
    )


def within(s, n):
    return jnp.logical_and(s >= 0, s < n)


def span_at(index, size):
    return pl.ds(pl.multiple_of(index * size, size), size)


def scale_into(out_ref, w_ref, fac_ref, at, blocks, block):
    for b in range(blocks):
        rows = slice(b * block, (b + 1) * block)
        for c in range(0, w_ref.shape[1], block):
            cols = slice(at + c, at + c + block)
            weight = w_ref[rows, c : c + block].astype(jnp.float32)
            out_ref[rows, cols] = (weight * fac_ref[b : b + 1, cols]).astype(jnp.bfloat16)


def head_kernel(
    n_f, n_t, share, block, pieces, pair_ref, wq_ref, wk_ref, wv_ref, fac_ref, q_ref, kv_ref,
    w_scr, hid, mine, px, up_in, down_in, acc,
    hid_send, hid_recv, side_send, pair_send, pair_recv,
    up_send, up_recv, down_send, down_recv, kv_send, kv_recv,
):
    f = lax.axis_index("fsdp")
    t = lax.axis_index("tp")
    n_z = n_f // CORES
    z, core = f // CORES, lax.rem(f, CORES)
    partner = z * CORES + (CORES - 1 - core)
    above, below = lax.rem(f + CORES, n_f), lax.rem(f - CORES + n_f, n_f)
    here = pair_ref.shape[1]
    slab = wq_ref.shape[0]
    quarter = here // n_t
    part = here // share
    q_cols, k_cols = wq_ref.shape[1], wk_ref.shape[1]
    blocks = slab // block
    side = [lax.rem(t + k, n_t) for k in range(n_t)]
    group, mate = f // share, lax.rem(f, share)

    def order(s):
        return lax.rem(s + n_f // 4, n_f)

    def piece_copy(i):
        rows = span_at(t, quarter)
        return remote(
            pieces.at[i], hid.at[f, rows], hid_send.at[i], hid_recv.at[f, t], {"fsdp": i}
        )

    def beside_copy():
        return remote(
            pair_ref.at[1], hid.at[f], hid_send.at[partner], hid_recv.at[f, 0], {"fsdp": partner}
        )

    def side_copy(b, k):
        rows = span_at(t, quarter)
        return remote(
            hid.at[b, rows], hid.at[b, rows], side_send.at[b, k], hid_recv.at[b, t], {"tp": side[k]}
        )

    def pair_copy(b):
        return remote(
            mine.at[b, CORES - 1 - core], px.at[b], pair_send.at[b], pair_recv.at[b],
            {"fsdp": partner},
        )

    def up_copy(b, zz):
        return remote(
            px.at[b, zz], up_in.at[b, zz], up_send.at[b, zz], up_recv.at[b, zz], {"fsdp": above}
        )

    def down_copy(b, zz):
        return remote(
            px.at[b, zz], down_in.at[b, zz], down_send.at[b, zz], down_recv.at[b, zz],
            {"fsdp": below},
        )

    def kv_copy(b, source, k):
        rows = pl.ds(pl.multiple_of(b * here + source * part, part), part)
        return remote(
            kv_ref.at[:, rows], kv_ref.at[:, rows], kv_send.at[b, k], kv_recv.at[b, source],
            {"fsdp": group * share + lax.rem(mate + k, share)},
        )

    greet_all(n_f, n_t, f, t)
    beside_copy().start()
    for d in range(1, n_z):
        for c in range(CORES):

            @pl.when(z + d < n_z)
            def _():
                piece_copy(lax.rem((z + d) * CORES + c, n_f)).start()

            @pl.when(z - d >= 0)
            def _():
                piece_copy(lax.rem((z - d + n_z) * CORES + c, n_f)).start()

    hid[f] = pair_ref[0]
    scale_into(w_scr, wq_ref, fac_ref, 0, blocks, block)
    scale_into(w_scr, wk_ref, fac_ref, q_cols, blocks, block)
    scale_into(w_scr, wv_ref, fac_ref, q_cols + k_cols, blocks, block)

    ahead = 2
    pair_lag = ahead + 1
    last_lag = ahead + n_z

    def step(s, carry):
        @pl.when(within(s, n_f))
        def _():
            b = order(s)

            @pl.when(b // CORES != z)
            def _():
                piece_like(b, t).wait_recv()
                for k in range(1, n_t):
                    side_copy(b, k).start()

        @pl.when(within(s - ahead, n_f))
        def _():
            b = order(s - ahead)

            @pl.when(b == partner)
            def _():
                remote(
                    pair_ref.at[1], hid.at[b], hid_send.at[0], hid_recv.at[b, 0], {"fsdp": partner}
                ).wait_recv()

            @pl.when(b // CORES != z)
            def _():
                for k in range(1, n_t):
                    piece_like(b, side[k]).wait_recv()

            both = jnp.dot(hid[b], w_scr[...], preferred_element_type=jnp.float32).astype(
                jnp.bfloat16
            )
            for j in range(n_f):
                g, p = j // share, j % share
                spot = mine.at[b, j % CORES, j // CORES]
                spot[:here, :] = both[:, j * HD : (j + 1) * HD]
                rows = slice(p * part, (p + 1) * part)
                k_at = q_cols + g * HD
                v_at = q_cols + k_cols + g * HD
                spot[here : here + part, :] = both[rows, k_at : k_at + HD]
                spot[here + part :, :] = both[rows, v_at : v_at + HD]
            pair_copy(b).start()

        @pl.when(within(s - pair_lag, n_f))
        def _():
            b = order(s - pair_lag)
            pair_copy(b).wait_recv()
            for zz in range(n_z):
                px[b, zz] = (
                    px[b, zz].astype(jnp.float32) + mine[b, core, zz].astype(jnp.float32)
                ).astype(jnp.bfloat16)

        up_at = s - pair_lag - z

        @pl.when(within(up_at, n_f))
        def _():
            b = order(up_at)
            for zz in range(n_z - 1, 0, -1):

                @pl.when(zz > z)
                def _():
                    @pl.when(z > 0)
                    def _():
                        up_copy(b, zz).wait_recv()
                        px[b, zz] = (
                            px[b, zz].astype(jnp.float32) + up_in[b, zz].astype(jnp.float32)
                        ).astype(jnp.bfloat16)

                    up_copy(b, zz).start()

        down_at = s - pair_lag - (n_z - 1 - z)

        @pl.when(within(down_at, n_f))
        def _():
            b = order(down_at)
            for zz in range(n_z - 1):

                @pl.when(zz < z)
                def _():
                    @pl.when(z < n_z - 1)
                    def _():
                        down_copy(b, zz).wait_recv()
                        px[b, zz] = (
                            px[b, zz].astype(jnp.float32) + down_in[b, zz].astype(jnp.float32)
                        ).astype(jnp.bfloat16)

                    down_copy(b, zz).start()

        @pl.when(within(s - last_lag, n_f))
        def _():
            b = order(s - last_lag)
            acc[...] = px[b, z].astype(jnp.float32)

            @pl.when(z > 0)
            def _():
                up_copy(b, z).wait_recv()
                acc[...] += up_in[b, z].astype(jnp.float32)

            @pl.when(z < n_z - 1)
            def _():
                down_copy(b, z).wait_recv()
                acc[...] += down_in[b, z].astype(jnp.float32)

            q_ref[span_at(b, here), :] = acc[:here, :].astype(jnp.bfloat16)
            rows = pl.ds(pl.multiple_of(b * here + mate * part, part), part)
            kv_ref[0, rows, :] = acc[here : here + part, :].astype(jnp.bfloat16)
            kv_ref[1, rows, :] = acc[here + part :, :].astype(jnp.bfloat16)
            for k in range(1, share):
                kv_copy(b, mate, k).start()

        return carry

    def piece_like(b, source):
        rows = span_at(source, quarter)
        return remote(
            pieces.at[0], hid.at[b, rows], hid_send.at[0], hid_recv.at[b, source], {"fsdp": above}
        )

    lax.fori_loop(0, n_f + last_lag, step, 0)

    def finish(b, carry):
        for k in range(1, share):
            kv_copy(b, lax.rem(mate - k + share, share), k).wait_recv()
            kv_copy(b, mate, k).wait_send()
        pair_copy(b).wait_send()

        @pl.when(b // CORES != z)
        def _():
            piece_copy(b).wait_send()
            for k in range(1, n_t):
                side_copy(b, k).wait_send()

        for zz in range(n_z):

            @pl.when(zz > z)
            def _():
                up_copy(b, zz).wait_send()

            @pl.when(zz < z)
            def _():
                down_copy(b, zz).wait_send()

        return carry

    lax.fori_loop(0, n_f, finish, 0)
    beside_copy().wait_send()


def arrange_kernel(n_f, owner_ref, place_ref, h_ref, pieces_ref, pair_ref, sem):
    quarter, slab = pieces_ref.shape[1], pieces_ref.shape[2]

    def columns(i):
        return pl.ds(pl.multiple_of(owner_ref[i] * slab, HD), slab)

    copies = []
    rows = pl.ds(pl.multiple_of(place_ref[0] * quarter, quarter), quarter)
    for k in range(2):
        source = h_ref.at[:, columns(place_ref[1 + k])]
        copies.append(pltpu.make_async_copy(source, pair_ref.at[k], sem.at[n_f + k]))
    for i in range(n_f):
        source = h_ref.at[rows, columns(i)]
        copies.append(pltpu.make_async_copy(source, pieces_ref.at[i], sem.at[i]))
    for copy in copies:
        copy.start()
    for copy in copies:
        copy.wait()


def arrange(n_f, n_t, slab, owner, hidden):
    f = lax.axis_index("fsdp")
    t = lax.axis_index("tp")
    here = hidden.shape[0]
    place = jnp.stack([t, f, f // CORES * CORES + (CORES - 1 - lax.rem(f, CORES))])
    whole = pl.BlockSpec(memory_space=VMEM)
    return pl.pallas_call(
        partial(arrange_kernel, n_f),
        out_shape=(
            jax.ShapeDtypeStruct((n_f, here // n_t, slab), hidden.dtype),
            jax.ShapeDtypeStruct((2, here, slab), hidden.dtype),
        ),
        in_specs=[pl.BlockSpec(memory_space=SMEM)] * 2 + [pl.BlockSpec(memory_space=pl.ANY)],
        out_specs=(whole, whole),
        scratch_shapes=[DMA((n_f + 2,))],
        name="arrange",
    )(owner, place, hidden)


def head(n_f, n_t, share, block, pieces, pair, w_query, w_key, w_value, factor):
    here = pair.shape[1]
    slab = w_query.shape[0]
    n_z = n_f // CORES
    cols = w_query.shape[1] + 2 * w_key.shape[1]
    packed = here + 2 * (here // share)
    tokens = here * n_f
    whole = pl.BlockSpec(memory_space=VMEM)
    return pl.pallas_call(
        partial(head_kernel, n_f, n_t, share, block),
        out_shape=(
            jax.ShapeDtypeStruct((tokens, HD), jnp.bfloat16),
            jax.ShapeDtypeStruct((2, tokens, HD), jnp.bfloat16),
        ),
        in_specs=[whole] * 6,
        out_specs=(whole, whole),
        scratch_shapes=[
            VMEM((slab, cols), jnp.bfloat16),
            VMEM((n_f, here, slab), jnp.bfloat16),
            VMEM((n_f, CORES, n_z, packed, HD), jnp.bfloat16),
            VMEM((n_f, n_z, packed, HD), jnp.bfloat16),
            VMEM((n_f, n_z, packed, HD), jnp.bfloat16),
            VMEM((n_f, n_z, packed, HD), jnp.bfloat16),
            VMEM((packed, HD), jnp.float32),
            DMA((n_f,)),
            DMA((n_f, n_t)),
            DMA((n_f, n_t)),
            DMA((n_f,)),
            DMA((n_f,)),
            DMA((n_f, n_z)),
            DMA((n_f, n_z)),
            DMA((n_f, n_z)),
            DMA((n_f, n_z)),
            DMA((n_f, share)),
            DMA((n_f, share)),
        ],
        compiler_params=pltpu.CompilerParams(
            collective_id=0, has_side_effects=True, vmem_limit_bytes=62 * 1024 * 1024
        ),
        name="project_and_sum",
    )(pieces, pair, w_query, w_key, w_value, factor)


def attend_kernel(inv_root, key_rows, q_ref, k_ref, v_ref, out_ref):
    i = pl.program_id(0)
    rows = q_ref.shape[0]
    query = q_ref[...]

    def step(j, state, masked):
        row_max, row_sum, accum = state
        at = pl.ds(pl.multiple_of(j * key_rows, key_rows), key_rows)
        scores = (
            lax.dot_general(
                query, k_ref[at, :], (((1,), (1,)), ((), ())), preferred_element_type=jnp.float32
            )
            * inv_root
        )
        if masked:
            q_pos = lax.broadcasted_iota(jnp.int32, scores.shape, 0)
            k_pos = lax.broadcasted_iota(jnp.int32, scores.shape, 1)
            scores = jnp.where(q_pos >= k_pos, scores, neg_large)
        new_max = jnp.maximum(row_max, jnp.max(scores, axis=1, keepdims=True))
        rescale = jnp.exp(row_max - new_max)
        weights = jnp.exp(scores - new_max)
        row_sum = row_sum * rescale + jnp.sum(weights, axis=1, keepdims=True)
        accum = accum * rescale + jnp.dot(
            weights.astype(jnp.bfloat16), v_ref[at, :], preferred_element_type=jnp.float32
        )
        return (new_max, row_sum, accum)

    state = (
        jnp.full((rows, 1), neg_large, jnp.float32),
        jnp.zeros((rows, 1), jnp.float32),
        jnp.zeros((rows, HD), jnp.float32),
    )
    state = step(i, state, True)
    _, row_sum, accum = lax.fori_loop(0, i, lambda j, s: step(j, s, False), state)
    out_ref[...] = (accum / row_sum).astype(jnp.bfloat16)


def tail_kernel(
    n_f, n_t, block, inverse_ref, c_ref, w_ref, fac_ref, out_ref,
    w_scr, ctx, y, got, total, slabs, fin,
    line_send, line_recv, sum_send, sum_recv, slab_send, slab_recv, last_send, last_recv,
):
    f = lax.axis_index("fsdp")
    t = lax.axis_index("tp")
    n_z = n_f // CORES
    z, core = f // CORES, lax.rem(f, CORES)
    partner = z * CORES + (CORES - 1 - core)
    above, below = lax.rem(f + CORES, n_f), lax.rem(f - CORES + n_f, n_f)
    here = c_ref.shape[0] // n_f
    slab = w_ref.shape[1]
    quarter = here // n_t
    per = n_f // n_t
    blocks = w_ref.shape[0] // block
    side = [lax.rem(t + k, n_t) for k in range(n_t)]

    def order(s):
        return lax.rem(s * 3, n_f)

    def line_copy(i, zz, to, which):
        rows = span_at(i, here)
        h = lax.rem(zz + n_z, n_z) * CORES + core
        return remote(
            ctx.at[h, rows], ctx.at[h, rows], line_send.at[i, h // CORES, which],
            line_recv.at[i, h], {"fsdp": to},
        )

    def line_wait(i, h):
        rows = span_at(i, here)
        remote(
            ctx.at[h, rows], ctx.at[h, rows], line_send.at[i, 0, 0], line_recv.at[i, h],
            {"fsdp": partner},
        ).wait_recv()

    def sum_copy(i, k):
        return remote(
            y.at[i, side[k]], got.at[i, k - 1], sum_send.at[i, k - 1], sum_recv.at[i, k - 1],
            {"tp": side[k]},
        )

    def slab_copy(i):
        return remote(total.at[i], slabs.at[f], slab_send.at[i], slab_recv.at[f], {"fsdp": i})

    def last_copy(k):
        return remote(
            fin.at[side[k]], out_ref.at[span_at(t, quarter)], last_send.at[k - 1],
            last_recv.at[k - 1], {"tp": side[k]},
        )

    ctx[f] = c_ref[...]
    w_scr[...] = jnp.zeros_like(w_scr)
    scale_into(w_scr, w_ref, fac_ref, 0, blocks, block)
    greet_all(n_f, n_t, f, t)

    def relay(s, d):
        @pl.when(within(s - d, n_f))
        def _():
            i = order(s - d)

            @pl.when(z - d >= 0)
            def _():
                zz = lax.rem(z - d + n_z, n_z)
                line_wait(i, zz * CORES + core)

                @pl.when(z < n_z - 1)
                def _():
                    line_copy(i, zz, above, 1).start()

                line_copy(i, zz, partner, 0).start()

            @pl.when(z + d < n_z)
            def _():
                zz = lax.rem(z + d, n_z)
                line_wait(i, zz * CORES + core)

                @pl.when(z > 0)
                def _():
                    line_copy(i, zz, below, 2).start()

                line_copy(i, zz, partner, 0).start()

    def step(s, carry):
        @pl.when(within(s, n_f))
        def _():
            i = order(s)

            @pl.when(z < n_z - 1)
            def _():
                line_copy(i, z, above, 1).start()

            @pl.when(z > 0)
            def _():
                line_copy(i, z, below, 2).start()

            line_copy(i, z, partner, 0).start()

        for d in range(1, n_z):
            relay(s, d)

        @pl.when(within(s - n_z, n_f))
        def _():
            i = order(s - n_z)
            for zz in range(n_z):
                line_wait(i, zz * CORES + (CORES - 1 - core))
            context = jnp.concatenate([ctx[h, span_at(i, here)] for h in range(n_f)], axis=1)
            part = jnp.dot(context, w_scr[...], preferred_element_type=jnp.float32).astype(
                jnp.bfloat16
            )
            for r in range(n_t):
                y[i, r] = part[r * quarter : (r + 1) * quarter, :slab]
            for k in range(1, n_t):
                sum_copy(i, k).start()

        @pl.when(within(s - n_z - 1, n_f))
        def _():
            i = order(s - n_z - 1)
            summed = y[i, t].astype(jnp.float32)
            for k in range(1, n_t):
                sum_copy(i, k).wait_recv()
                summed = summed + got[i, k - 1].astype(jnp.float32)
            total[i] = summed.astype(jnp.bfloat16)

            @pl.when(i == f)
            def _():
                slabs[i] = total[i]

            @pl.when(i != f)
            def _():
                slab_copy(i).start()

        return carry

    lax.fori_loop(0, n_f + n_z + 1, step, 0)

    for d in range(1, n_f):
        source = lax.rem(f + d, n_f)
        remote(
            total.at[0], slabs.at[source], slab_send.at[0], slab_recv.at[source], {"fsdp": source}
        ).wait_recv()
    for j in range(n_f):
        fin[j // per, :, (j % per) * slab : (j % per + 1) * slab] = slabs[inverse_ref[j]]
    for k in range(1, n_t):
        last_copy(k).start()
    out_ref[span_at(t, quarter), :] = fin[t]

    def finish(i, carry):
        @pl.when(i != f)
        def _():
            slab_copy(i).wait_send()

        for k in range(1, n_t):
            sum_copy(i, k).wait_send()
        for zz in range(n_z):
            line_copy(i, zz, partner, 0).wait_send()

            @pl.when(jnp.logical_and(zz <= z, z < n_z - 1))
            def _():
                line_copy(i, zz, above, 1).wait_send()

            @pl.when(jnp.logical_and(zz >= z, z > 0))
            def _():
                line_copy(i, zz, below, 2).wait_send()

        return carry

    lax.fori_loop(0, n_f, finish, 0)
    for k in range(1, n_t):
        source = lax.rem(t - k + n_t, n_t)
        remote(
            fin.at[0], out_ref.at[span_at(source, quarter)], last_send.at[k - 1],
            last_recv.at[k - 1], {"tp": side[1]},
        ).wait_recv()
        last_copy(k).wait_send()


def tail(n_f, n_t, block, inverse, context, w_out, factor):
    tokens = context.shape[0]
    here = tokens // n_f
    quarter = here // n_t
    slab = w_out.shape[1]
    wide = slab * n_f // n_t
    n_z = n_f // CORES
    whole = pl.BlockSpec(memory_space=VMEM)
    return pl.pallas_call(
        partial(tail_kernel, n_f, n_t, block),
        out_shape=jax.ShapeDtypeStruct((here, wide), jnp.bfloat16),
        in_specs=[pl.BlockSpec(memory_space=SMEM)] + [whole] * 3,
        out_specs=whole,
        scratch_shapes=[
            VMEM((w_out.shape[0], slab + -slab % 256), jnp.bfloat16),
            VMEM((n_f, tokens, HD), jnp.bfloat16),
            VMEM((n_f, n_t, quarter, slab), jnp.bfloat16),
            VMEM((n_f, n_t - 1, quarter, slab), jnp.bfloat16),
            VMEM((n_f, quarter, slab), jnp.bfloat16),
            VMEM((n_f, quarter, slab), jnp.bfloat16),
            VMEM((n_t, quarter, wide), jnp.bfloat16),
            DMA((n_f, n_z, 3)),
            DMA((n_f, n_f)),
            DMA((n_f, n_t - 1)),
            DMA((n_f, n_t - 1)),
            DMA((n_f,)),
            DMA((n_f,)),
            DMA((n_t - 1,)),
            DMA((n_t - 1,)),
        ],
        compiler_params=pltpu.CompilerParams(
            collective_id=1, has_side_effects=True, vmem_limit_bytes=56 * 1024 * 1024
        ),
        name="project_out_and_sum",
    )(inverse, context, w_out, factor)


def stationary_body(
    n_f, n_t, hidden, w_query, w_key, w_value, w_out, exp_query, exp_key, exp_value, exp_out, owner
):
    f = lax.axis_index("fsdp")
    t = lax.axis_index("tp")
    here, width = hidden.shape
    slab = w_query.shape[0]
    tokens = here * n_f
    block = width // exp_query.shape[0]
    slab_blocks = slab // block
    q_cols, k_cols = w_query.shape[1], w_key.shape[1]
    share = (q_cols // HD) // (k_cols // HD)
    logical = owner[f]

    def factors(exponents, cols):
        picked = lax.dynamic_slice(
            exponents, (logical * slab_blocks, t * (cols // block)), (slab_blocks, cols // block)
        )
        return jnp.repeat(jnp.exp2(picked.astype(jnp.float32)), block, axis=1)

    in_factor = jnp.concatenate(
        [factors(exp_query, q_cols), factors(exp_key, k_cols), factors(exp_value, k_cols)], axis=1
    )
    out_rows = w_out.shape[0] // block
    out_factor = jnp.repeat(
        jnp.exp2(
            lax.dynamic_slice(
                exp_out, (t * out_rows, logical * slab_blocks), (out_rows, slab_blocks)
            ).astype(jnp.float32)
        ),
        block,
        axis=1,
    )
    in_factor = jnp.pad(in_factor, ((0, -slab_blocks % 8), (0, 0)))
    out_factor = jnp.pad(out_factor, ((0, -out_rows % 8), (0, -slab % 256)))

    pieces, pair = arrange(n_f, n_t, slab, owner, hidden)
    query, kv = head(
        n_f, n_t, share, block, pieces, pair, w_query, w_key, w_value, in_factor
    )
    tile = here
    context = pl.pallas_call(
        partial(attend_kernel, 1.0 / math.sqrt(HD), tile),
        grid=(tokens // tile,),
        out_shape=jax.ShapeDtypeStruct((tokens, HD), jnp.bfloat16),
        in_specs=[
            pl.BlockSpec((tile, HD), lambda i: (i, 0)),
            pl.BlockSpec((pl.squeezed, tokens, HD), lambda i: (0, 0, 0)),
            pl.BlockSpec((pl.squeezed, tokens, HD), lambda i: (1, 0, 0)),
        ],
        out_specs=pl.BlockSpec((tile, HD), lambda i: (i, 0)),
        compiler_params=pltpu.CompilerParams(vmem_limit_bytes=48 * 1024 * 1024),
        name="attend",
    )(query, kv, kv)

    slab_ids = jnp.arange(n_f, dtype=jnp.int32)
    inverse = jnp.sum(
        slab_ids[:, None] * (owner[:, None] == slab_ids[None, :]).astype(jnp.int32), axis=0
    )
    return tail(n_f, n_t, block, inverse, context, w_out, out_factor)


def solution(mesh):
    n_f, n_t = mesh.shape["fsdp"], mesh.shape["tp"]

    def body(*arrays):
        hidden, w_query, w_key = arrays[0], arrays[1], arrays[2]
        heads, kv_heads = w_query.shape[1] // HD, w_key.shape[1] // HD
        share = heads // kv_heads
        fits = (
            heads == n_f
            and n_f % n_t == 0
            and n_f % CORES == 0
            and hidden.shape[0] % (16 * n_t) == 0
            and hidden.shape[0] % (16 * share) == 0
        )
        if fits:
            return stationary_body(n_f, n_t, *arrays)
        return gather_body(*arrays)

    placed = (
        P("fsdp", None),
        P("fsdp", "tp"),
        P("fsdp", "tp"),
        P("fsdp", "tp"),
        P("tp", "fsdp"),
        P(),
        P(),
        P(),
        P(),
        P(),
    )
    return jax.shard_map(
        body, mesh=mesh, in_specs=placed, out_specs=P("fsdp", "tp"), check_vma=False
    )
```

time: 466 us -> 307 us (0.66)
  the two profiles are of different devices: /device:TPU:25 before, /device:TPU:0 now
where the time goes in v1:
time: 307 us
  Pallas kernels  294 us (96%)
  local copies, waits for them, and re-layouts  7.8 us (3%)
  other arithmetic  4.28 us (1%)
    pallas_call x1, Pallas kernels, head(): pl.pallas_call(partial(head_kernel, n_f, n_t, share, block), out_shape=(j...  151 us
    pallas_call x1, Pallas kernels, tail(): pl.pallas_call(partial(tail_kernel, n_f, n_t, block), out_shape=jax.Shape...  118 us
    pallas_call x1, Pallas kernels, stationary_body(): pl.pallas_call(partial(attend_kernel, 1.0 / math.sqrt(HD), tile), grid=(t...  20.4 us
    unnamed x15, local copies, waits for them, and re-layouts  6.16 us

profile of v1, /device:TPU:0, one launch (start us, length us, event | category | flops | bytes accessed | tf_op | source)
XLA Modules:
  0.0 306.9 jit_solution(14518543181182713954)
XLA Ops:
  0.0 0.7 pad_add_fusion.place_ref
  0.7 0.0 copy-start.3
  0.7 4.2 %arrange.1 = (bf16[8,96,896]{2,1,0:T(8,128)(2,1)}, bf16[2,384,896]{2,1,0:T(8,128)(2,1)}) custom-call(s32[8]{0:T(128)} %owner_ref.1, s32[3]{0:T(128)} %pad_add_fusion.place_ref, bf16[384,7168]{1,0:T(8,128)(2,1)} %h_ref.1), custom_call_target="tpu_custom_call" | custom-call | tf_op jit(solution)/shard_map/arrange/pallas_call | solution.py:463
  4.8 0.0 copy-done.3
  4.9 0.6 dynamic_slice.15
  6.0 0.8 multiply_exponential_fusion.1
  6.8 0.1 copy.15
  6.9 0.1 broadcast_bitcast_fusion.1
  7.0 0.8 multiply_exponential_fusion.2
  7.7 0.1 copy.17
  7.8 0.1 broadcast_bitcast_fusion.2
  7.9 0.1 copy.16
  8.0 0.1 broadcast_bitcast_fusion.3
  8.1 0.6 select_maximum_fusion.fac_ref
  8.7 151.2 %project_and_sum.1 = (bf16[3072,128]{1,0:T(8,128)(2,1)}, bf16[2,3072,128]{2,1,0:T(8,128)(2,1)}) custom-call(bf16[8,96,896]{2,1,0:T(8,128)(2,1)} %get-tuple-element.9.pieces, bf16[2,384,896]{2,1,0:T(8,128)(2,1)} %get-tuple-element.10.pair_ref, bf16[896,1024]{1,0:T(8,128)(2,1)} %wq_ref.1, bf16[896,256]{1,0:T(8,128)(2,1)} %wk_ref.1, bf16[896,256]{1,0:T(8,128)(2,1)} %wv_ref.1, ...), custom_call_target="tpu_custom_call" | custom-call | tf_op jit(solution)/shard_map/project_and_sum/pallas_call | solution.py:484
  159.9 0.0 copy-start
  159.9 1.4 copy-done
  161.3 0.0 copy-start.2
  161.3 1.1 copy-done.2
  162.5 20.4 %attend.1.c_ref = bf16[3072,128]{1,0:T(8,128)(2,1)S(1)} custom-call(bf16[3072,128]{1,0:T(8,128)(2,1)S(1)} %copy-done.2, bf16[2,3072,128]{2,1,0:T(8,128)(2,1)S(1)} %copy-done, bf16[2,3072,128]{2,1,0:T(8,128)(2,1)S(1)} %copy-done), custom_call_target="tpu_custom_call" | custom-call | tf_op jit(solution)/shard_map/attend/pallas_call | solution.py:811
  182.9 0.0 copy-start.1
  182.9 0.9 copy-done.1
  183.7 0.8 multiply_exponential_fusion
  184.5 0.1 copy.18
  184.6 0.1 broadcast_bitcast_fusion
  184.7 0.6 pad.9.fac_ref
  185.3 0.7 select_reduce_fusion.inverse_ref
  185.9 118.4 %project_out_and_sum.1 = bf16[384,1792]{1,0:T(8,128)(2,1)} custom-call(s32[8]{0:T(128)} %select_reduce_fusion.inverse_ref, bf16[3072,128]{1,0:T(8,128)(2,1)} %copy-done.1, bf16[1024,896]{1,0:T(8,128)(2,1)} %w_ref.1, f32[8,1024]{1,0:T(8,128)} %pad.9.fac_ref), custom_call_target="tpu_custom_call" | custom-call | tf_op jit(solution)/shard_map/project_out_and_sum/pallas_call | solution.py:741
  304.3 2.5 copy.29
  (3 shorter events, 0.0 us)
Async XLA Ops:
  0.7 4.2 %copy-start.3 = (s32[8]{0:T(128)S(1)}, s32[8]{0:T(128)}, u32[]{:S(2)}) copy-start(s32[8]{0:T(128)} %owner_ref.1) | copy-start | bytes 100
  159.9 1.4 copy-start
  161.3 1.1 copy-start.2
  182.9 0.9 copy-start.1

commit v2 on v1

--- a/solution.py
+++ b/solution.py
@@ -158,6 +158,8 @@
 SMEM = pltpu.SMEM
 DMA = pltpu.SemaphoreType.DMA
 CORES = 2
+LINE = 4
+SIDE = 2
 
 
 def greet(peers):
@@ -223,8 +225,11 @@
     side = [lax.rem(t + k, n_t) for k in range(n_t)]
     group, mate = f // share, lax.rem(f, share)
 
-    def order(s):
-        return lax.rem(s + n_f // 4, n_f)
+    middle = 1 - (z == 0).astype(jnp.int32) - (z == n_z - 1).astype(jnp.int32)
+    upper = z // (n_z // 2)
+
+    def turned(b):
+        return b + upper * (n_f - 1 - 2 * b)
 
     def piece_copy(i):
         rows = span_at(t, quarter)
@@ -285,64 +290,112 @@
     scale_into(w_scr, wk_ref, fac_ref, q_cols, blocks, block)
     scale_into(w_scr, wv_ref, fac_ref, q_cols + k_cols, blocks, block)
 
-    ahead = 2
-    pair_lag = ahead + 1
-    last_lag = ahead + n_z
+    def piece_like(b, source):
+        rows = span_at(source, quarter)
+        return remote(
+            pieces.at[0], hid.at[b, rows], hid_send.at[0], hid_recv.at[b, source], {"fsdp": above}
+        )
+
+    def pass_on(b):
+        piece_like(b, t).wait_recv()
+        for k in range(1, n_t):
+            side_copy(b, k).start()
+
+    def project(b):
+        @pl.when(b == partner)
+        def _():
+            remote(
+                pair_ref.at[1], hid.at[b], hid_send.at[0], hid_recv.at[b, 0], {"fsdp": partner}
+            ).wait_recv()
+
+        @pl.when(b // CORES != z)
+        def _():
+            for k in range(1, n_t):
+                piece_like(b, side[k]).wait_recv()
+
+        both = jnp.dot(hid[b], w_scr[...], preferred_element_type=jnp.float32).astype(
+            jnp.bfloat16
+        )
+        for j in range(n_f):
+            g, p = j // share, j % share
+            spot = mine.at[b, j % CORES, j // CORES]
+            spot[:here, :] = both[:, j * HD : (j + 1) * HD]
+            rows = slice(p * part, (p + 1) * part)
+            k_at = q_cols + g * HD
+            v_at = q_cols + k_cols + g * HD
+            spot[here : here + part, :] = both[rows, k_at : k_at + HD]
+            spot[here + part :, :] = both[rows, v_at : v_at + HD]
+        pair_copy(b).start()
+
+    def join_pair(b):
+        pair_copy(b).wait_recv()
+        for zz in range(n_z):
+            px[b, zz] = (
+                px[b, zz].astype(jnp.float32) + mine[b, core, zz].astype(jnp.float32)
+            ).astype(jnp.bfloat16)
+
+    def first_slot(s, work):
+        at = s - middle
+
+        @pl.when(within(at, n_f - middle * (n_f // 2)))
+        def _():
+            work(turned(at))
+
+    def second_slot(s, work):
+        at = s - 2
+
+        @pl.when(jnp.logical_and(middle == 1, within(at, n_f // 2)))
+        def _():
+            work(turned(n_f - 1 - at))
+
+    def close(b):
+        acc[...] = px[b, z].astype(jnp.float32)
+
+        @pl.when(z > 0)
+        def _():
+            up_copy(b, z).wait_recv()
+            acc[...] += up_in[b, z].astype(jnp.float32)
+
+        @pl.when(z < n_z - 1)
+        def _():
+            down_copy(b, z).wait_recv()
+            acc[...] += down_in[b, z].astype(jnp.float32)
+
+        q_ref[span_at(b, here), :] = acc[:here, :].astype(jnp.bfloat16)
+        rows = pl.ds(pl.multiple_of(b * here + mate * part, part), part)
+        kv_ref[0, rows, :] = acc[here : here + part, :].astype(jnp.bfloat16)
+        kv_ref[1, rows, :] = acc[here + part :, :].astype(jnp.bfloat16)
+        for k in range(1, share):
+            kv_copy(b, mate, k).start()
+
+    @pl.when(middle == 1)
+    def _():
+        for c in range(CORES):
+            pass_on(turned(c))
+        for c in range(CORES):
+            pass_on(turned(3 * CORES - 1 - c))
 
     def step(s, carry):
-        @pl.when(within(s, n_f))
-        def _():
-            b = order(s)
-
-            @pl.when(b // CORES != z)
-            def _():
-                piece_like(b, t).wait_recv()
-                for k in range(1, n_t):
-                    side_copy(b, k).start()
-
-        @pl.when(within(s - ahead, n_f))
-        def _():
-            b = order(s - ahead)
-
-            @pl.when(b == partner)
-            def _():
-                remote(
-                    pair_ref.at[1], hid.at[b], hid_send.at[0], hid_recv.at[b, 0], {"fsdp": partner}
-                ).wait_recv()
-
-            @pl.when(b // CORES != z)
-            def _():
-                for k in range(1, n_t):
-                    piece_like(b, side[k]).wait_recv()
-
-            both = jnp.dot(hid[b], w_scr[...], preferred_element_type=jnp.float32).astype(
-                jnp.bfloat16
-            )
-            for j in range(n_f):
-                g, p = j // share, j % share
-                spot = mine.at[b, j % CORES, j // CORES]
-                spot[:here, :] = both[:, j * HD : (j + 1) * HD]
-                rows = slice(p * part, (p + 1) * part)
-                k_at = q_cols + g * HD
-                v_at = q_cols + k_cols + g * HD
-                spot[here : here + part, :] = both[rows, k_at : k_at + HD]
-                spot[here + part :, :] = both[rows, v_at : v_at + HD]
-            pair_copy(b).start()
-
-        @pl.when(within(s - pair_lag, n_f))
-        def _():
-            b = order(s - pair_lag)
-            pair_copy(b).wait_recv()
-            for zz in range(n_z):
-                px[b, zz] = (
-                    px[b, zz].astype(jnp.float32) + mine[b, core, zz].astype(jnp.float32)
-                ).astype(jnp.bfloat16)
-
-        up_at = s - pair_lag - z
+        first_slot(s, project)
+        second_slot(s, project)
+
+        @pl.when(jnp.logical_and(middle == 0, within(s, n_f - CORES)))
+        def _():
+            pass_on(turned(s + CORES))
+
+        @pl.when(jnp.logical_and(middle == 1, s == 1))
+        def _():
+            for c in range(CORES):
+                pass_on(turned(n_f - 1 - c))
+
+        first_slot(s - 1, join_pair)
+        second_slot(s - 1, join_pair)
+
+        up_at = s - 1 - z
 
         @pl.when(within(up_at, n_f))
         def _():
-            b = order(up_at)
+            b = up_at
             for zz in range(n_z - 1, 0, -1):
 
                 @pl.when(zz > z)
@@ -356,11 +409,11 @@
 
                     up_copy(b, zz).start()
 
-        down_at = s - pair_lag - (n_z - 1 - z)
+        down_at = s - 1 - (n_z - 1 - z)
 
         @pl.when(within(down_at, n_f))
         def _():
-            b = order(down_at)
+            b = n_f - 1 - down_at
             for zz in range(n_z - 1):
 
                 @pl.when(zz < z)
@@ -374,37 +427,24 @@
 
                     down_copy(b, zz).start()
 
-        @pl.when(within(s - last_lag, n_f))
-        def _():
-            b = order(s - last_lag)
-            acc[...] = px[b, z].astype(jnp.float32)
-
-            @pl.when(z > 0)
-            def _():
-                up_copy(b, z).wait_recv()
-                acc[...] += up_in[b, z].astype(jnp.float32)
-
-            @pl.when(z < n_z - 1)
-            def _():
-                down_copy(b, z).wait_recv()
-                acc[...] += down_in[b, z].astype(jnp.float32)
-
-            q_ref[span_at(b, here), :] = acc[:here, :].astype(jnp.bfloat16)
-            rows = pl.ds(pl.multiple_of(b * here + mate * part, part), part)
-            kv_ref[0, rows, :] = acc[here : here + part, :].astype(jnp.bfloat16)
-            kv_ref[1, rows, :] = acc[here + part :, :].astype(jnp.bfloat16)
-            for k in range(1, share):
-                kv_copy(b, mate, k).start()
+        one = middle * (n_f + 2 - s) + (1 - middle) * (n_f - 1 - 2 * (s - n_f))
+        first_close = n_f - 2 * middle
+
+        @pl.when(jnp.logical_and(s >= first_close, one >= 0))
+        def _():
+            close(turned(one))
+
+        two = middle * (s - 2) + (1 - middle) * (one - 1)
+
+        @pl.when(
+            jnp.logical_and(s >= first_close + middle, jnp.logical_and(two >= 0, two < n_f))
+        )
+        def _():
+            close(turned(two))
 
         return carry
 
-    def piece_like(b, source):
-        rows = span_at(source, quarter)
-        return remote(
-            pieces.at[0], hid.at[b, rows], hid_send.at[0], hid_recv.at[b, source], {"fsdp": above}
-        )
-
-    lax.fori_loop(0, n_f + last_lag, step, 0)
+    lax.fori_loop(0, n_f + n_z, step, 0)
 
     def finish(b, carry):
         for k in range(1, share):
@@ -516,46 +556,41 @@
     )(pieces, pair, w_query, w_key, w_value, factor)
 
 
-def attend_kernel(inv_root, key_rows, q_ref, k_ref, v_ref, out_ref):
-    i = pl.program_id(0)
-    rows = q_ref.shape[0]
-    query = q_ref[...]
-
-    def step(j, state, masked):
+def attend_tile(scale, i, here, q_ref, kv_ref):
+    query = q_ref[span_at(i, here), :]
+
+    def chunk(j, state, masked):
         row_max, row_sum, accum = state
-        at = pl.ds(pl.multiple_of(j * key_rows, key_rows), key_rows)
-        scores = (
-            lax.dot_general(
-                query, k_ref[at, :], (((1,), (1,)), ((), ())), preferred_element_type=jnp.float32
-            )
-            * inv_root
+        at = span_at(j, here)
+        scores = lax.dot_general(
+            query, kv_ref[0, at, :], (((1,), (1,)), ((), ())), preferred_element_type=jnp.float32
         )
         if masked:
             q_pos = lax.broadcasted_iota(jnp.int32, scores.shape, 0)
             k_pos = lax.broadcasted_iota(jnp.int32, scores.shape, 1)
             scores = jnp.where(q_pos >= k_pos, scores, neg_large)
         new_max = jnp.maximum(row_max, jnp.max(scores, axis=1, keepdims=True))
-        rescale = jnp.exp(row_max - new_max)
-        weights = jnp.exp(scores - new_max)
+        rescale = jnp.exp2((row_max - new_max) * scale)
+        weights = jnp.exp2((scores - new_max) * scale)
         row_sum = row_sum * rescale + jnp.sum(weights, axis=1, keepdims=True)
         accum = accum * rescale + jnp.dot(
-            weights.astype(jnp.bfloat16), v_ref[at, :], preferred_element_type=jnp.float32
+            weights.astype(jnp.bfloat16), kv_ref[1, at, :], preferred_element_type=jnp.float32
         )
         return (new_max, row_sum, accum)
 
     state = (
-        jnp.full((rows, 1), neg_large, jnp.float32),
-        jnp.zeros((rows, 1), jnp.float32),
-        jnp.zeros((rows, HD), jnp.float32),
-    )
-    state = step(i, state, True)
-    _, row_sum, accum = lax.fori_loop(0, i, lambda j, s: step(j, s, False), state)
-    out_ref[...] = (accum / row_sum).astype(jnp.bfloat16)
+        jnp.full((here, 1), neg_large, jnp.float32),
+        jnp.zeros((here, 1), jnp.float32),
+        jnp.zeros((here, HD), jnp.float32),
+    )
+    state = chunk(i, state, True)
+    _, row_sum, accum = lax.fori_loop(0, i, lambda j, s: chunk(j, s, False), state)
+    return (accum / row_sum).astype(jnp.bfloat16)
 
 
 def tail_kernel(
-    n_f, n_t, block, inverse_ref, c_ref, w_ref, fac_ref, out_ref,
-    w_scr, ctx, y, got, total, slabs, fin,
+    n_f, n_t, block, inverse_ref, q_ref, kv_ref, w_ref, fac_ref, out_ref,
+    w_scr, ctx, y, half_in, full_in, total, slabs, fin,
     line_send, line_recv, sum_send, sum_recv, slab_send, slab_recv, last_send, last_recv,
 ):
     f = lax.axis_index("fsdp")
@@ -564,12 +599,16 @@
     z, core = f // CORES, lax.rem(f, CORES)
     partner = z * CORES + (CORES - 1 - core)
     above, below = lax.rem(f + CORES, n_f), lax.rem(f - CORES + n_f, n_f)
-    here = c_ref.shape[0] // n_f
+    here = q_ref.shape[0] // n_f
+    scale = 1.0 / (math.sqrt(HD) * math.log(2.0))
     slab = w_ref.shape[1]
     quarter = here // n_t
     per = n_f // n_t
+    half = quarter // 2
     blocks = w_ref.shape[0] // block
     side = [lax.rem(t + k, n_t) for k in range(n_t)]
+    along = [t + 1 - 2 * lax.rem(t, 2), lax.rem(t + n_t // 2, n_t)]
+    across = n_t - 1 - t
 
     def order(s):
         return lax.rem(s * 3, n_f)
@@ -589,10 +628,17 @@
             {"fsdp": partner},
         ).wait_recv()
 
-    def sum_copy(i, k):
-        return remote(
-            y.at[i, side[k]], got.at[i, k - 1], sum_send.at[i, k - 1], sum_recv.at[i, k - 1],
-            {"tp": side[k]},
+    def half_copy(i, k):
+        rows = slice(k * half, (k + 1) * half)
+        return remote(
+            y.at[i, across, rows], half_in.at[i, k], sum_send.at[i, k], sum_recv.at[i, k],
+            {"tp": along[k]},
+        )
+
+    def full_copy(i, k):
+        return remote(
+            y.at[i, along[k]], full_in.at[i, k], sum_send.at[i, 2 + k], sum_recv.at[i, 2 + k],
+            {"tp": along[k]},
         )
 
     def slab_copy(i):
@@ -604,7 +650,6 @@
             last_recv.at[k - 1], {"tp": side[k]},
         )
 
-    ctx[f] = c_ref[...]
     w_scr[...] = jnp.zeros_like(w_scr)
     scale_into(w_scr, w_ref, fac_ref, 0, blocks, block)
     greet_all(n_f, n_t, f, t)
@@ -640,6 +685,7 @@
         @pl.when(within(s, n_f))
         def _():
             i = order(s)
+            ctx[f, span_at(i, here), :] = attend_tile(scale, i, here, q_ref, kv_ref)
 
             @pl.when(z < n_z - 1)
             def _():
@@ -665,48 +711,64 @@
             )
             for r in range(n_t):
                 y[i, r] = part[r * quarter : (r + 1) * quarter, :slab]
+            for k in range(2):
+                half_copy(i, k).start()
+
+        @pl.when(within(s - n_z - 1, n_f))
+        def _():
+            i = order(s - n_z - 1)
+            for k in range(2):
+                half_copy(i, k).wait_recv()
+                rows = slice(k * half, (k + 1) * half)
+                to = along[1 - k]
+                y[i, to, rows] = (
+                    y[i, to, rows].astype(jnp.float32) + half_in[i, k].astype(jnp.float32)
+                ).astype(jnp.bfloat16)
+                full_copy(i, 1 - k).start()
+
+        @pl.when(within(s - n_z - 2, n_f))
+        def _():
+            i = order(s - n_z - 2)
+            summed = y[i, t].astype(jnp.float32)
+            for k in range(2):
+                full_copy(i, k).wait_recv()
+                summed = summed + full_in[i, k].astype(jnp.float32)
+            total[i] = summed.astype(jnp.bfloat16)
+
+            @pl.when(i == f)
+            def _():
+                slabs[i] = total[i]
+
+            @pl.when(i != f)
+            def _():
+                slab_copy(i).start()
+
+        @pl.when(jnp.logical_and(within(s - n_z - 3, n_f), order(s + n_f - n_z - 3) == f))
+        def _():
+            for d in range(1, n_f):
+                source = lax.rem(f + d, n_f)
+                remote(
+                    total.at[0], slabs.at[source], slab_send.at[0], slab_recv.at[source],
+                    {"fsdp": source},
+                ).wait_recv()
+            for j in range(n_f):
+                fin[j // per, :, (j % per) * slab : (j % per + 1) * slab] = slabs[inverse_ref[j]]
             for k in range(1, n_t):
-                sum_copy(i, k).start()
-
-        @pl.when(within(s - n_z - 1, n_f))
-        def _():
-            i = order(s - n_z - 1)
-            summed = y[i, t].astype(jnp.float32)
-            for k in range(1, n_t):
-                sum_copy(i, k).wait_recv()
-                summed = summed + got[i, k - 1].astype(jnp.float32)
-            total[i] = summed.astype(jnp.bfloat16)
-
-            @pl.when(i == f)
-            def _():
-                slabs[i] = total[i]
-
-            @pl.when(i != f)
-            def _():
-                slab_copy(i).start()
+                last_copy(k).start()
+            out_ref[span_at(t, quarter), :] = fin[t]
 
         return carry
 
-    lax.fori_loop(0, n_f + n_z + 1, step, 0)
-
-    for d in range(1, n_f):
-        source = lax.rem(f + d, n_f)
-        remote(
-            total.at[0], slabs.at[source], slab_send.at[0], slab_recv.at[source], {"fsdp": source}
-        ).wait_recv()
-    for j in range(n_f):
-        fin[j // per, :, (j % per) * slab : (j % per + 1) * slab] = slabs[inverse_ref[j]]
-    for k in range(1, n_t):
-        last_copy(k).start()
-    out_ref[span_at(t, quarter), :] = fin[t]
+    lax.fori_loop(0, n_f + n_z + 3, step, 0)
 
     def finish(i, carry):
         @pl.when(i != f)
         def _():
             slab_copy(i).wait_send()
 
-        for k in range(1, n_t):
-            sum_copy(i, k).wait_send()
+        for k in range(2):
+            half_copy(i, k).wait_send()
+            full_copy(i, k).wait_send()
         for zz in range(n_z):
             line_copy(i, zz, partner, 0).wait_send()
 
@@ -730,8 +792,8 @@
         last_copy(k).wait_send()
 
 
-def tail(n_f, n_t, block, inverse, context, w_out, factor):
-    tokens = context.shape[0]
+def tail(n_f, n_t, block, inverse, query, kv, w_out, factor):
+    tokens = query.shape[0]
     here = tokens // n_f
     quarter = here // n_t
     slab = w_out.shape[1]
@@ -741,20 +803,21 @@
     return pl.pallas_call(
         partial(tail_kernel, n_f, n_t, block),
         out_shape=jax.ShapeDtypeStruct((here, wide), jnp.bfloat16),
-        in_specs=[pl.BlockSpec(memory_space=SMEM)] + [whole] * 3,
+        in_specs=[pl.BlockSpec(memory_space=SMEM)] + [whole] * 4,
         out_specs=whole,
         scratch_shapes=[
             VMEM((w_out.shape[0], slab + -slab % 256), jnp.bfloat16),
             VMEM((n_f, tokens, HD), jnp.bfloat16),
             VMEM((n_f, n_t, quarter, slab), jnp.bfloat16),
-            VMEM((n_f, n_t - 1, quarter, slab), jnp.bfloat16),
+            VMEM((n_f, 2, quarter // 2, slab), jnp.bfloat16),
+            VMEM((n_f, 2, quarter, slab), jnp.bfloat16),
             VMEM((n_f, quarter, slab), jnp.bfloat16),
             VMEM((n_f, quarter, slab), jnp.bfloat16),
             VMEM((n_t, quarter, wide), jnp.bfloat16),
             DMA((n_f, n_z, 3)),
             DMA((n_f, n_f)),
-            DMA((n_f, n_t - 1)),
-            DMA((n_f, n_t - 1)),
+            DMA((n_f, 4)),
+            DMA((n_f, 4)),
             DMA((n_f,)),
             DMA((n_f,)),
             DMA((n_t - 1,)),
@@ -764,7 +827,7 @@
             collective_id=1, has_side_effects=True, vmem_limit_bytes=56 * 1024 * 1024
         ),
         name="project_out_and_sum",
-    )(inverse, context, w_out, factor)
+    )(inverse, query, kv, w_out, factor)
 
 
 def stationary_body(
@@ -807,26 +870,11 @@
     query, kv = head(
         n_f, n_t, share, block, pieces, pair, w_query, w_key, w_value, in_factor
     )
-    tile = here
-    context = pl.pallas_call(
-        partial(attend_kernel, 1.0 / math.sqrt(HD), tile),
-        grid=(tokens // tile,),
-        out_shape=jax.ShapeDtypeStruct((tokens, HD), jnp.bfloat16),
-        in_specs=[
-            pl.BlockSpec((tile, HD), lambda i: (i, 0)),
-            pl.BlockSpec((pl.squeezed, tokens, HD), lambda i: (0, 0, 0)),
-            pl.BlockSpec((pl.squeezed, tokens, HD), lambda i: (1, 0, 0)),
-        ],
-        out_specs=pl.BlockSpec((tile, HD), lambda i: (i, 0)),
-        compiler_params=pltpu.CompilerParams(vmem_limit_bytes=48 * 1024 * 1024),
-        name="attend",
-    )(query, kv, kv)
-
     slab_ids = jnp.arange(n_f, dtype=jnp.int32)
     inverse = jnp.sum(
         slab_ids[:, None] * (owner[:, None] == slab_ids[None, :]).astype(jnp.int32), axis=0
     )
-    return tail(n_f, n_t, block, inverse, context, w_out, out_factor)
+    return tail(n_f, n_t, block, inverse, query, kv, w_out, out_factor)
 
 
 def solution(mesh):
@@ -838,9 +886,10 @@
         share = heads // kv_heads
         fits = (
             heads == n_f
+            and n_t == SIDE * SIDE
             and n_f % n_t == 0
-            and n_f % CORES == 0
-            and hidden.shape[0] % (16 * n_t) == 0
+            and n_f == LINE * CORES
+            and hidden.shape[0] % (16 * SIDE * n_t) == 0
             and hidden.shape[0] % (16 * share) == 0
         )
         if fits:

time: 307 us -> 264 us (0.86)
  the two profiles are of different devices: /device:TPU:0 before, /device:TPU:17 now
where the time goes in v2:
time: 264 us
  Pallas kernels  254 us (96%)
  local copies, waits for them, and re-layouts  4.46 us (2%)
  other arithmetic  4.15 us (2%)
    pallas_call x1, Pallas kernels, head(): pl.pallas_call(partial(head_kernel, n_f, n_t, share, block), out_shape=(j...  126 us
    pallas_call x1, Pallas kernels, tail(): pl.pallas_call(partial(tail_kernel, n_f, n_t, block), out_shape=jax.Shape...  124 us

profile of v2, /device:TPU:17, one launch (start us, length us, event | category | flops | bytes accessed | tf_op | source)
XLA Modules:
  0.0 263.6 jit_solution(505789372393692100)
XLA Ops:
  0.0 0.6 pad_add_fusion.place_ref
  0.6 0.0 copy-start
  0.6 4.2 %arrange.1 = (bf16[8,96,896]{2,1,0:T(8,128)(2,1)}, bf16[2,384,896]{2,1,0:T(8,128)(2,1)}) custom-call(s32[8]{0:T(128)} %owner_ref.1, s32[3]{0:T(128)} %pad_add_fusion.place_ref, bf16[384,7168]{1,0:T(8,128)(2,1)} %h_ref.1), custom_call_target="tpu_custom_call" | custom-call | tf_op jit(solution)/shard_map/arrange/pallas_call | solution.py:503
  4.8 0.0 copy-done
  4.8 0.7 dynamic_slice.15
  6.1 0.8 multiply_exponential_fusion.1
  6.9 0.1 copy.15
  7.0 0.1 broadcast_bitcast_fusion.1
  7.1 0.8 multiply_exponential_fusion.2
  7.8 0.1 copy.17
  7.9 0.1 broadcast_bitcast_fusion.2
  8.0 0.1 copy.16
  8.1 0.1 broadcast_bitcast_fusion.3
  8.2 0.6 select_maximum_fusion.fac_ref
  8.8 125.8 %project_and_sum.1 = (bf16[3072,128]{1,0:T(8,128)(2,1)}, bf16[2,3072,128]{2,1,0:T(8,128)(2,1)}) custom-call(bf16[8,96,896]{2,1,0:T(8,128)(2,1)} %get-tuple-element.9.pieces, bf16[2,384,896]{2,1,0:T(8,128)(2,1)} %get-tuple-element.10.pair_ref, bf16[896,1024]{1,0:T(8,128)(2,1)} %wq_ref.1, bf16[896,256]{1,0:T(8,128)(2,1)} %wk_ref.1, bf16[896,256]{1,0:T(8,128)(2,1)} %wv_ref.1, ...), custom_call_target="tpu_custom_call" | custom-call | tf_op jit(solution)/shard_map/project_and_sum/pallas_call | solution.py:524
  134.6 0.8 multiply_exponential_fusion
  135.4 0.1 copy.18
  135.5 0.1 broadcast_bitcast_fusion
  135.6 0.6 pad.9.fac_ref
  136.2 0.6 select_reduce_fusion.inverse_ref
  136.7 124.3 %project_out_and_sum.1 = bf16[384,1792]{1,0:T(8,128)(2,1)} custom-call(s32[8]{0:T(128)} %select_reduce_fusion.inverse_ref, bf16[3072,128]{1,0:T(8,128)(2,1)} %get-tuple-element.11.q_ref, bf16[2,3072,128]{2,1,0:T(8,128)(2,1)} %get-tuple-element.12.kv_ref, bf16[1024,896]{1,0:T(8,128)(2,1)} %w_ref.1, f32[8,1024]{1,0:T(8,128)} %pad.9.fac_ref), custom_call_target="tpu_custom_call" | custom-call | tf_op jit(solution)/shard_map/project_out_and_sum/pallas_call | solution.py:803
  261.1 2.5 copy.29
  (3 shorter events, 0.0 us)
Async XLA Ops:
  0.6 4.2 %copy-start = (s32[8]{0:T(128)S(1)}, s32[8]{0:T(128)}, u32[]{:S(2)}) copy-start(s32[8]{0:T(128)} %owner_ref.1) | copy-start | bytes 100

commit v3 on v2

v3 whole, which is shorter than its diff:
```python
from functools import partial
import math

import jax
import jax.numpy as jnp
from jax import lax
from jax.experimental import pallas as pl
from jax.experimental.pallas import tpu as pltpu
from jax.sharding import PartitionSpec as P

HQ = 32
HK = 8
HD = 128


neg_large = -1e30


def block_factor(exponents, row_start, row_count, col_start, col_count, block_size):
    repeated = jnp.repeat(exponents, block_size, axis=0)
    picked = lax.dynamic_slice_in_dim(repeated, row_start, row_count, 0)
    repeated = jnp.repeat(picked, block_size, axis=1)
    picked = lax.dynamic_slice_in_dim(repeated, col_start, col_count, 1)
    return jnp.exp2(picked.astype(jnp.float32))


def block_update(state, query_half, pos_half, keys_part, values_part, key_pos, inv_root):
    row_max, row_sum, accum = state
    causal = pos_half[:, None] >= key_pos[None, :]
    scores = (
        jnp.einsum("tgjd,ngd->gjtn", query_half, keys_part, preferred_element_type=jnp.float32)
        * inv_root
    )
    scores = jnp.where(causal, scores, neg_large)
    new_max = jnp.maximum(row_max, jnp.max(scores, axis=3))
    rescale = jnp.exp(row_max - new_max)
    weights = jnp.where(causal, jnp.exp(scores - new_max[..., None]), 0.0)
    row_sum = row_sum * rescale + jnp.sum(weights, axis=3)
    accum = accum * rescale[..., None] + jnp.einsum(
        "gjtn,ngd->gjtd",
        weights.astype(jnp.bfloat16),
        values_part,
        preferred_element_type=jnp.float32,
    )
    return (new_max, row_sum, accum)


def keep_state(state):
    return state


def gather_body(hidden, w_query, w_key, w_value, w_out, exp_query, exp_key, exp_value, exp_out, owner):
    fsdp_index = lax.axis_index("fsdp")
    tp_index = lax.axis_index("tp")
    slab_rows = w_query.shape[0]
    groups = owner.shape[0]
    tokens = hidden.shape[0]
    model_width = hidden.shape[1]
    block_size = model_width // exp_query.shape[0]
    slab_start = owner[fsdp_index] * slab_rows
    query_cols = w_query.shape[1]
    key_cols = w_key.shape[1]

    def scaled_rows(weight, exponents):
        col_count = weight.shape[1]
        factor = block_factor(
            exponents, slab_start, slab_rows, tp_index * col_count, col_count, block_size
        )
        return (weight.astype(jnp.float32) * factor).astype(jnp.bfloat16)

    query_local = scaled_rows(w_query, exp_query)
    key_local = scaled_rows(w_key, exp_key)
    value_local = scaled_rows(w_value, exp_value)
    out_rows = w_out.shape[0]
    out_factor = block_factor(
        exp_out, tp_index * out_rows, out_rows, slab_start, slab_rows, block_size
    )
    out_local = (w_out.astype(jnp.float32) * out_factor).astype(jnp.bfloat16)
    arranged = jnp.take(hidden.reshape(tokens, groups, slab_rows), owner, axis=1).reshape(
        tokens, model_width
    )
    pieces = (
        lax.all_gather(query_local, "fsdp", axis=0, tiled=True),
        lax.all_gather(key_local, "fsdp", axis=0, tiled=True),
        lax.all_gather(value_local, "fsdp", axis=0, tiled=True),
    )
    query_sum, key_sum, value_sum = tuple(
        (jnp.dot(arranged, weight, preferred_element_type=jnp.float32) for weight in pieces)
    )
    query = query_sum.astype(jnp.bfloat16)
    key_here = key_sum.astype(jnp.bfloat16)
    value_here = value_sum.astype(jnp.bfloat16)
    half_rows = tokens // 2
    local_pos = fsdp_index * tokens + jnp.arange(tokens, dtype=jnp.int32)
    group_size = HQ // HK
    kv_heads = key_cols // HD
    query_halves = query.reshape(2, half_rows, kv_heads, group_size, HD)
    pos_halves = local_pos.reshape(2, half_rows)
    pos_top = jnp.max(pos_halves, axis=1)
    inv_root = 1.0 / math.sqrt(HD)
    one_state = (
        jnp.full((kv_heads, group_size, half_rows), neg_large, jnp.float32),
        jnp.zeros((kv_heads, group_size, half_rows), jnp.float32),
        jnp.zeros((kv_heads, group_size, half_rows, HD), jnp.float32),
    )
    offset = jnp.int32(0)
    key_piece = lax.all_gather(key_here, "fsdp", axis=0, tiled=True)
    value_piece = lax.all_gather(value_here, "fsdp", axis=0, tiled=True)
    states = list((one_state, one_state))
    piece_rows = key_piece.shape[0]
    for block_low in range(0, piece_rows, 1024):
        block_high = min(block_low + 1024, piece_rows)
        width_here = block_high - block_low
        keys_part = key_piece[block_low:block_high].reshape(width_here, kv_heads, HD)
        values_part = value_piece[block_low:block_high].reshape(width_here, kv_heads, HD)
        key_pos = offset + block_low + jnp.arange(width_here, dtype=jnp.int32)
        for attend_which in range(2):
            update = partial(
                block_update,
                query_half=query_halves[attend_which],
                pos_half=pos_halves[attend_which],
                keys_part=keys_part,
                values_part=values_part,
                key_pos=key_pos,
                inv_root=inv_root,
            )
            states[attend_which] = lax.cond(
                offset + block_low <= pos_top[attend_which],
                update,
                keep_state,
                states[attend_which],
            )
    final_states = tuple(states)
    context_parts = []
    for which in range(2):
        row_max, row_sum, accum = final_states[which]
        part_context = (accum / row_sum[..., None]).astype(jnp.bfloat16)
        context_parts.append(part_context.transpose(2, 0, 1, 3).reshape(half_rows, query_cols))
    context = jnp.concatenate(context_parts, axis=0)
    column_terms = jnp.dot(
        context,
        lax.all_gather(out_local, "fsdp", axis=1, tiled=True),
        preferred_element_type=jnp.float32,
    )
    slab_ids = jnp.arange(groups, dtype=jnp.int32)
    inverse = jnp.sum(
        slab_ids[:, None] * (owner[:, None] == slab_ids[None, :]).astype(jnp.int32), axis=0
    )
    ordered = jnp.take(column_terms.reshape(tokens, groups, slab_rows), inverse, axis=1).reshape(
        tokens, model_width
    )
    result = lax.psum_scatter(ordered.astype(jnp.bfloat16), "tp", scatter_dimension=1, tiled=True)
    return result


MESH = pl.DeviceIdType.MESH
VMEM = pltpu.VMEM
SMEM = pltpu.SMEM
DMA = pltpu.SemaphoreType.DMA
CORES = 2
LINE = 4
SIDE = 2
SPLIT = 2


def greet(peers):
    barrier = pltpu.get_barrier_semaphore()
    for device in peers:
        pl.semaphore_signal(barrier, inc=1, device_id=device, device_id_type=MESH)
    pl.semaphore_wait(barrier, len(peers))


def greet_all(n_f, n_t, f, t):
    greet(
        [{"fsdp": lax.rem(f + d, n_f)} for d in range(1, n_f)]
        + [{"tp": lax.rem(t + k, n_t)} for k in range(1, n_t)]
    )


def remote(src, dst, send, recv, device):
    return pltpu.make_async_remote_copy(
        src_ref=src,
        dst_ref=dst,
        send_sem=send,
        recv_sem=recv,
        device_id=device,
        device_id_type=MESH,
    )


def within(s, n):
    return jnp.logical_and(s >= 0, s < n)


def span_at(index, size):
    return pl.ds(pl.multiple_of(index * size, size), size)


def arrange_kernel(
    n_f, n_t, block, owner_ref, eq_hbm, ek_hbm, ev_hbm, eo_hbm, h_ref,
    pieces_ref, pair_ref, in_ref, out_ref, inverse_ref, eq_ref, ek_ref, ev_ref, eo_ref, sem, small,
):
    f = lax.axis_index("fsdp")
    t = lax.axis_index("tp")
    partner = f // CORES * CORES + (CORES - 1 - lax.rem(f, CORES))
    rows, slab = pieces_ref.shape[2], pieces_ref.shape[3]
    here = pair_ref.shape[1]

    def columns(i):
        return pl.ds(pl.multiple_of(owner_ref[i] * slab, HD), slab)

    tables = [
        pltpu.make_async_copy(source, target, small.at[k])
        for k, (source, target) in enumerate(
            ((eq_hbm, eq_ref), (ek_hbm, ek_ref), (ev_hbm, ev_ref), (eo_hbm, eo_ref))
        )
    ]
    for copy in tables:
        copy.start()
    copies = []
    for k, device in enumerate((f, partner)):
        source = h_ref.at[:, columns(device)]
        copies.append(pltpu.make_async_copy(source, pair_ref.at[k], sem.at[n_f, k]))
    for i in range(n_f):
        for p in range(SPLIT):
            start = pl.multiple_of(p * (here // SPLIT) + t * rows, rows)
            source = h_ref.at[pl.ds(start, rows), columns(i)]
            copies.append(pltpu.make_async_copy(source, pieces_ref.at[i, p], sem.at[i, p]))
    for copy in copies:
        copy.start()

    logical = owner_ref[f]
    blocks = slab // block

    def spread_out(exponents, first, width):
        shape = (exponents.shape[1], width)
        block_of = lax.broadcasted_iota(jnp.int32, shape, 1) // block + first
        chosen = lax.broadcasted_iota(jnp.int32, shape, 0) == block_of
        return jnp.dot(
            jnp.exp2(exponents.astype(jnp.float32)),
            chosen.astype(jnp.float32),
            preferred_element_type=jnp.float32,
        )

    for copy in tables:
        copy.wait()
    at = 0
    for ref in (eq_ref, ek_ref, ev_ref):
        cols = ref.shape[1] // n_t
        picked = ref[pl.ds(logical * blocks, blocks), :]
        in_ref[:blocks, at : at + cols * block] = spread_out(picked, t * cols, cols * block)
        at += cols * block
    picked = eo_ref[span_at(t, eo_ref.shape[0] // n_t), :]
    out_ref[: picked.shape[0], :] = spread_out(picked, logical * blocks, slab)
    for i in range(n_f):
        inverse_ref[owner_ref[i]] = i
    for copy in copies:
        copy.wait()


def arrange(n_f, n_t, block, owner, hidden, exponents, in_cols, out_rows, slab):
    here = hidden.shape[0]
    blocks = slab // block
    whole = pl.BlockSpec(memory_space=VMEM)
    small = pl.BlockSpec(memory_space=SMEM)
    return pl.pallas_call(
        partial(arrange_kernel, n_f, n_t, block),
        out_shape=(
            jax.ShapeDtypeStruct((n_f, SPLIT, here // (n_t * SPLIT), slab), hidden.dtype),
            jax.ShapeDtypeStruct((2, here, slab), hidden.dtype),
            jax.ShapeDtypeStruct((blocks + -blocks % 8, in_cols), jnp.float32),
            jax.ShapeDtypeStruct((out_rows // block + -(out_rows // block) % 8, slab), jnp.float32),
            jax.ShapeDtypeStruct((n_f,), jnp.int32),
        ),
        in_specs=[small] + [pl.BlockSpec(memory_space=pl.ANY)] * 5,
        out_specs=(whole, whole, whole, whole, small),
        scratch_shapes=[VMEM(e.shape, e.dtype) for e in exponents]
        + [DMA((n_f + 1, SPLIT)), DMA((len(exponents),))],
        name="arrange",
    )(owner, *exponents, hidden)


def scale_in_place(w_scr, fac_ref, block):
    for b in range(w_scr.shape[0] // block):
        rows = slice(b * block, (b + 1) * block)
        for c in range(0, fac_ref.shape[1], block):
            cols = slice(c, c + block)
            weight = w_scr[rows, cols].astype(jnp.float32)
            w_scr[rows, cols] = (weight * fac_ref[b : b + 1, cols]).astype(jnp.bfloat16)


def attend_tile(scale, i, here, q_ref, kv_ref):
    query = q_ref[span_at(i, here), :]

    def chunk(at, state, masked):
        row_max, row_sum, accum = state
        scores = lax.dot_general(
            query, kv_ref[0, at, :], (((1,), (1,)), ((), ())), preferred_element_type=jnp.float32
        )
        if masked:
            q_pos = lax.broadcasted_iota(jnp.int32, scores.shape, 0)
            k_pos = lax.broadcasted_iota(jnp.int32, scores.shape, 1)
            scores = jnp.where(q_pos >= k_pos, scores, neg_large)
        new_max = jnp.maximum(row_max, jnp.max(scores, axis=1, keepdims=True))
        rescale = jnp.exp2((row_max - new_max) * scale)
        weights = jnp.exp2((scores - new_max) * scale)
        row_sum = row_sum * rescale + jnp.sum(weights, axis=1, keepdims=True)
        accum = accum * rescale + jnp.dot(
            weights.astype(jnp.bfloat16), kv_ref[1, at, :], preferred_element_type=jnp.float32
        )
        return (new_max, row_sum, accum)

    state = (
        jnp.full((here, 1), neg_large, jnp.float32),
        jnp.zeros((here, 1), jnp.float32),
        jnp.zeros((here, HD), jnp.float32),
    )
    state = chunk(span_at(i, here), state, True)
    wide = SPAN * here
    left = lax.rem(i, SPAN)
    state = lax.fori_loop(0, left, lambda j, s: chunk(span_at(i - 1 - j, here), s, False), state)
    _, row_sum, accum = lax.fori_loop(
        0, i // SPAN, lambda j, s: chunk(span_at(j, wide), s, False), state
    )
    return (accum / row_sum).astype(jnp.bfloat16)


SPAN = 2
PROJECT = 2
PAIR = PROJECT + 1
CLOSE = PAIR + LINE - 1
ATTEND = CLOSE + 1


def layer_kernel(
    n_f, n_t, share, block, inverse_ref, pieces, pair_ref, wq_ref, wk_ref, wv_ref, wo_ref,
    fac_ref, faco_ref, out_ref,
    w_scr, wo_scr, hid, mine, px, up_in, down_in, acc, q_scr, kv_scr,
    ctx, y, half_in, full_in, total, slabs_even, slabs_odd, fin, load,
    hid_send, hid_recv, side_send, pair_send, pair_recv,
    up_send, up_recv, down_send, down_recv, kv_send, kv_recv,
    line_send, line_recv, sum_send, sum_recv, slab_send, slab_recv, last_send, last_recv,
):
    f = lax.axis_index("fsdp")
    t = lax.axis_index("tp")
    n_z = n_f // CORES
    z, core = f // CORES, lax.rem(f, CORES)
    partner = z * CORES + (CORES - 1 - core)
    above, below = lax.rem(f + CORES, n_f), lax.rem(f - CORES + n_f, n_f)
    n_b = n_f * SPLIT
    here, slab = pair_ref.shape[1] // SPLIT, pair_ref.shape[2]
    quarter = here // n_t
    part = here // share
    per = n_f // n_t
    q_cols, k_cols = wq_ref.shape[1], wk_ref.shape[1]
    scale = 1.0 / (math.sqrt(HD) * math.log(2.0))
    side = [lax.rem(t + k, n_t) for k in range(n_t)]
    along = [t + 1 - 2 * lax.rem(t, 2), lax.rem(t + n_t // 2, n_t)]
    across = n_t - 1 - t
    group, mate = f // share, lax.rem(f, share)
    slabs = (slabs_even, slabs_odd)

    def piece_copy(i, p):
        b = f * SPLIT + p
        rows = span_at(t, quarter)
        return remote(
            pieces.at[i, p], hid.at[b, rows], hid_send.at[i, p], hid_recv.at[b, t], {"fsdp": i}
        )

    def beside_copy(p):
        b = f * SPLIT + p
        rows = slice(p * here, (p + 1) * here)
        return remote(
            pair_ref.at[1, rows], hid.at[b], hid_send.at[partner, p], hid_recv.at[b, 0],
            {"fsdp": partner},
        )

    def side_copy(b, k):
        rows = span_at(t, quarter)
        return remote(
            hid.at[b, rows], hid.at[b, rows], side_send.at[b, k], hid_recv.at[b, t], {"tp": side[k]}
        )

    def pair_copy(b):
        return remote(
            mine.at[lax.rem(b, 2), CORES - 1 - core], px.at[b], pair_send.at[b], pair_recv.at[b],
            {"fsdp": partner},
        )

    def up_copy(b, zz):
        return remote(
            px.at[b, zz], up_in.at[b, zz], up_send.at[b, zz], up_recv.at[b, zz], {"fsdp": above}
        )

    def down_copy(b, zz):
        return remote(
            px.at[b, zz], down_in.at[b, zz], down_send.at[b, zz], down_recv.at[b, zz],
            {"fsdp": below},
        )

    def kv_copy(b, source, k):
        rows = pl.ds(pl.multiple_of(b * here + source * part, part), part)
        return remote(
            kv_scr.at[:, rows], kv_scr.at[:, rows], kv_send.at[b, k], kv_recv.at[b, source],
            {"fsdp": group * share + lax.rem(mate + k, share)},
        )

    def line_copy(i, zz, to, which):
        rows = span_at(i, here)
        h = lax.rem(zz + n_z, n_z) * CORES + core
        return remote(
            ctx.at[h, rows], ctx.at[h, rows], line_send.at[i, h // CORES, which],
            line_recv.at[i, h], {"fsdp": to},
        )

    def line_wait(i, h):
        rows = span_at(i, here)
        remote(
            ctx.at[h, rows], ctx.at[h, rows], line_send.at[i, 0, 0], line_recv.at[i, h],
            {"fsdp": partner},
        ).wait_recv()

    def either(i):
        first = lax.rem(i, 2)
        return along[0] + first * (along[1] - along[0]), along[1] + first * (along[0] - along[1])

    def diagonal_copy(i):
        return remote(
            y.at[i, across], half_in.at[i], sum_send.at[i, 2], sum_recv.at[i, 2],
            {"tp": either(i)[0]},
        )

    def full_copy(i, k):
        return remote(
            y.at[i, along[k]], full_in.at[i, k], sum_send.at[i, k], sum_recv.at[i, k],
            {"tp": along[k]},
        )

    def slab_copy(i, p):
        return remote(
            total.at[i], slabs[p].at[f], slab_send.at[i], slab_recv.at[f, p], {"fsdp": i // SPLIT}
        )

    def out_rows(p, source):
        return pl.ds(pl.multiple_of(p * here + source * quarter, quarter), quarter)

    def last_copy(p, k):
        return remote(
            fin.at[p, side[k]], out_ref.at[out_rows(p, t)], last_send.at[p, k - 1],
            last_recv.at[p, k - 1], {"tp": side[k]},
        )

    loads = [
        pltpu.make_async_copy(wq_ref, w_scr.at[:, :q_cols], load.at[0]),
        pltpu.make_async_copy(wk_ref, w_scr.at[:, q_cols : q_cols + k_cols], load.at[1]),
        pltpu.make_async_copy(wv_ref, w_scr.at[:, q_cols + k_cols :], load.at[2]),
        pltpu.make_async_copy(wo_ref, wo_scr.at[:, :slab], load.at[3]),
    ]
    for copy in loads:
        copy.start()
    greet_all(n_f, n_t, f, t)
    for p in range(SPLIT):
        beside_copy(p).start()
    for p in range(SPLIT):
        for d in range(n_z - 1, 0, -1):
            for c in range(CORES):

                @pl.when(z + d < n_z)
                def _():
                    piece_copy(lax.rem((z + d) * CORES + c, n_f), p).start()

                @pl.when(z - d >= 0)
                def _():
                    piece_copy(lax.rem((z - d + n_z) * CORES + c, n_f), p).start()

    for p in range(SPLIT):
        hid[f * SPLIT + p] = pair_ref[0, p * here : (p + 1) * here]
    wo_scr[:, slab:] = jnp.zeros((wo_scr.shape[0], wo_scr.shape[1] - slab), jnp.bfloat16)
    for copy in loads:
        copy.wait()
    scale_in_place(w_scr, fac_ref, block)
    scale_in_place(wo_scr, faco_ref, block)

    def piece_like(b, source):
        rows = span_at(source, quarter)
        return remote(
            pieces.at[0, 0], hid.at[b, rows], hid_send.at[0, 0], hid_recv.at[b, source],
            {"fsdp": above},
        )

    def pass_on(b):
        piece_like(b, t).wait_recv()
        for k in range(1, n_t):
            side_copy(b, k).start()

    def project(b):
        @pl.when(b // SPLIT == partner)
        def _():
            remote(
                pair_ref.at[1, :here], hid.at[b], hid_send.at[0, 0], hid_recv.at[b, 0],
                {"fsdp": partner},
            ).wait_recv()

        @pl.when(b // (SPLIT * CORES) != z)
        def _():
            for k in range(1, n_t):
                piece_like(b, side[k]).wait_recv()

        @pl.when(b >= 2)
        def _():
            pair_copy(b - 2).wait_send()

        both = jnp.dot(hid[b], w_scr[...], preferred_element_type=jnp.float32).astype(
            jnp.bfloat16
        )
        for j in range(n_f):
            g, p = j // share, j % share
            spot = mine.at[lax.rem(b, 2), j % CORES, j // CORES]
            spot[:here, :] = both[:, j * HD : (j + 1) * HD]
            rows = slice(p * part, (p + 1) * part)
            k_at = q_cols + g * HD
            v_at = q_cols + k_cols + g * HD
            spot[here : here + part, :] = both[rows, k_at : k_at + HD]
            spot[here + part :, :] = both[rows, v_at : v_at + HD]
        pair_copy(b).start()

    def join_pair(b):
        pair_copy(b).wait_recv()
        for zz in range(n_z):
            px[b, zz] = (
                px[b, zz].astype(jnp.float32) + mine[lax.rem(b, 2), core, zz].astype(jnp.float32)
            ).astype(jnp.bfloat16)

    def close(b):
        acc[...] = px[b, z].astype(jnp.float32)

        @pl.when(z > 0)
        def _():
            up_copy(b, z).wait_recv()
            acc[...] += up_in[b, z].astype(jnp.float32)

        @pl.when(z < n_z - 1)
        def _():
            down_copy(b, z).wait_recv()
            acc[...] += down_in[b, z].astype(jnp.float32)

        q_scr[span_at(b, here), :] = acc[:here, :].astype(jnp.bfloat16)
        rows = pl.ds(pl.multiple_of(b * here + mate * part, part), part)
        kv_scr[0, rows, :] = acc[here : here + part, :].astype(jnp.bfloat16)
        kv_scr[1, rows, :] = acc[here + part :, :].astype(jnp.bfloat16)
        for k in range(1, share):
            kv_copy(b, mate, k).start()

    def relay(s, d):
        @pl.when(within(s - ATTEND - d, n_b))
        def _():
            i = s - ATTEND - d

            @pl.when(z - d >= 0)
            def _():
                zz = lax.rem(z - d + n_z, n_z)
                line_wait(i, zz * CORES + core)

                @pl.when(z < n_z - 1)
                def _():
                    line_copy(i, zz, above, 1).start()

                line_copy(i, zz, partner, 0).start()

            @pl.when(z + d < n_z)
            def _():
                zz = lax.rem(z + d, n_z)
                line_wait(i, zz * CORES + core)

                @pl.when(z > 0)
                def _():
                    line_copy(i, zz, below, 2).start()

                line_copy(i, zz, partner, 0).start()

    def step(s, carry):
        @pl.when(within(s, n_b))
        def _():
            @pl.when(s // (SPLIT * CORES) != z)
            def _():
                pass_on(s)

        @pl.when(within(s - PAIR, n_b))
        def _():
            join_pair(s - PAIR)

        up_at = s - PAIR - z

        @pl.when(within(up_at, n_b))
        def _():
            b = up_at
            for zz in range(n_z - 1, 0, -1):

                @pl.when(zz > z)
                def _():
                    @pl.when(z > 0)
                    def _():
                        up_copy(b, zz).wait_recv()
                        px[b, zz] = (
                            px[b, zz].astype(jnp.float32) + up_in[b, zz].astype(jnp.float32)
                        ).astype(jnp.bfloat16)

                    up_copy(b, zz).start()

        down_at = s - PAIR - (n_z - 1 - z)

        @pl.when(within(down_at, n_b))
        def _():
            b = down_at
            for zz in range(n_z - 1):

                @pl.when(zz < z)
                def _():
                    @pl.when(z < n_z - 1)
                    def _():
                        down_copy(b, zz).wait_recv()
                        px[b, zz] = (
                            px[b, zz].astype(jnp.float32) + down_in[b, zz].astype(jnp.float32)
                        ).astype(jnp.bfloat16)

                    down_copy(b, zz).start()

        @pl.when(within(s - PROJECT, n_b))
        def _():
            project(s - PROJECT)

        @pl.when(within(s - CLOSE, n_b))
        def _():
            close(s - CLOSE)

        for d in range(1, n_z):
            relay(s, d)

        @pl.when(within(s - ATTEND, n_b))
        def _():
            i = s - ATTEND
            for k in range(1, share):
                kv_copy(i, lax.rem(mate - k + share, share), k).wait_recv()
            ctx[f, span_at(i, here), :] = attend_tile(scale, i, here, q_scr, kv_scr)

            @pl.when(z < n_z - 1)
            def _():
                line_copy(i, z, above, 1).start()

            @pl.when(z > 0)
            def _():
                line_copy(i, z, below, 2).start()

            line_copy(i, z, partner, 0).start()

        @pl.when(within(s - ATTEND - n_z, n_b))
        def _():
            i = s - ATTEND - n_z
            for zz in range(n_z):
                line_wait(i, zz * CORES + (CORES - 1 - core))
            context = jnp.concatenate([ctx[h, span_at(i, here)] for h in range(n_f)], axis=1)
            part = jnp.dot(context, wo_scr[...], preferred_element_type=jnp.float32).astype(
                jnp.bfloat16
            )
            for r in range(n_t):
                y[i, r] = part[r * quarter : (r + 1) * quarter, :slab]
            diagonal_copy(i).start()

        @pl.when(within(s - ATTEND - n_z - 1, n_b))
        def _():
            i = s - ATTEND - n_z - 1
            diagonal_copy(i).wait_recv()
            to = either(i)[1]
            y[i, to] = (y[i, to].astype(jnp.float32) + half_in[i].astype(jnp.float32)).astype(
                jnp.bfloat16
            )
            for k in range(2):
                full_copy(i, k).start()

        @pl.when(within(s - ATTEND - n_z - 2, n_b))
        def _():
            i = s - ATTEND - n_z - 2
            summed = y[i, t].astype(jnp.float32)
            for k in range(2):
                full_copy(i, k).wait_recv()
                summed = summed + full_in[i, k].astype(jnp.float32)
            total[i] = summed.astype(jnp.bfloat16)

            for p in range(SPLIT):

                @pl.when(i == f * SPLIT + p)
                def _():
                    slabs[p][f] = total[i]

                @pl.when(jnp.logical_and(i // SPLIT != f, lax.rem(i, SPLIT) == p))
                def _():
                    slab_copy(i, p).start()

        for p in range(SPLIT):

            @pl.when(s - ATTEND - n_z - 3 == f * SPLIT + p)
            def _():
                for d in range(1, n_f):
                    source = lax.rem(f + d, n_f)
                    remote(
                        total.at[0], slabs[p].at[source], slab_send.at[0], slab_recv.at[source, p],
                        {"fsdp": source},
                    ).wait_recv()
                for j in range(n_f):
                    cols = slice((j % per) * slab, (j % per + 1) * slab)
                    fin[p, j // per, :, cols] = slabs[p][inverse_ref[j]]
                for k in range(1, n_t):
                    last_copy(p, k).start()
                out_ref[out_rows(p, t), :] = fin[p, t]

        return carry

    lax.fori_loop(0, n_b + ATTEND + n_z + 3, step, 0)

    def finish_head(b, carry):
        for k in range(1, share):
            kv_copy(b, mate, k).wait_send()
        @pl.when(b >= n_b - 2)
        def _():
            pair_copy(b).wait_send()

        @pl.when(b // (SPLIT * CORES) != z)
        def _():
            piece_copy(b // SPLIT, lax.rem(b, SPLIT)).wait_send()
            for k in range(1, n_t):
                side_copy(b, k).wait_send()

        for zz in range(n_z):

            @pl.when(zz > z)
            def _():
                up_copy(b, zz).wait_send()

            @pl.when(zz < z)
            def _():
                down_copy(b, zz).wait_send()

        return carry

    lax.fori_loop(0, n_b, finish_head, 0)
    for p in range(SPLIT):
        beside_copy(p).wait_send()


    def finish(i, carry):
        @pl.when(i // SPLIT != f)
        def _():
            slab_copy(i, 0).wait_send()

        diagonal_copy(i).wait_send()
        for k in range(2):
            full_copy(i, k).wait_send()
        for zz in range(n_z):
            line_copy(i, zz, partner, 0).wait_send()

            @pl.when(jnp.logical_and(zz <= z, z < n_z - 1))
            def _():
                line_copy(i, zz, above, 1).wait_send()

            @pl.when(jnp.logical_and(zz >= z, z > 0))
            def _():
                line_copy(i, zz, below, 2).wait_send()

        return carry

    lax.fori_loop(0, n_b, finish, 0)
    for p in range(SPLIT):
        for k in range(1, n_t):
            source = lax.rem(t - k + n_t, n_t)
            remote(
                fin.at[p, 0], out_ref.at[out_rows(p, source)], last_send.at[p, k - 1],
                last_recv.at[p, k - 1], {"tp": side[1]},
            ).wait_recv()
            last_copy(p, k).wait_send()


def layer(n_f, n_t, share, block, inverse, pieces, pair, w_query, w_key, w_value, w_out, fac, faco):
    n_b = n_f * SPLIT
    here, slab = pair.shape[1] // SPLIT, pair.shape[2]
    quarter = here // n_t
    n_z = n_f // CORES
    cols = w_query.shape[1] + 2 * w_key.shape[1]
    packed = here + 2 * (here // share)
    tokens = here * n_b
    wide = slab * n_f // n_t
    whole = pl.BlockSpec(memory_space=VMEM)
    stay = pl.BlockSpec(memory_space=pl.ANY)
    small = jnp.bfloat16
    return pl.pallas_call(
        partial(layer_kernel, n_f, n_t, share, block),
        out_shape=jax.ShapeDtypeStruct((here * SPLIT, wide), small),
        in_specs=[pl.BlockSpec(memory_space=SMEM), whole, whole] + [stay] * 4 + [whole] * 2,
        out_specs=whole,
        scratch_shapes=[
            VMEM((slab, cols), small),
            VMEM((w_out.shape[0], slab + -slab % 256), small),
            VMEM((n_b, here, slab), small),
            VMEM((2, CORES, n_z, packed, HD), small),
            VMEM((n_b, n_z, packed, HD), small),
            VMEM((n_b, n_z, packed, HD), small),
            VMEM((n_b, n_z, packed, HD), small),
            VMEM((packed, HD), jnp.float32),
            VMEM((tokens, HD), small),
            VMEM((2, tokens, HD), small),
            VMEM((n_f, tokens, HD), small),
            VMEM((n_b, n_t, quarter, slab), small),
            VMEM((n_b, quarter, slab), small),
            VMEM((n_b, 2, quarter, slab), small),
            VMEM((n_b, quarter, slab), small),
            VMEM((n_f, quarter, slab), small),
            VMEM((n_f, quarter, slab), small),
            VMEM((SPLIT, n_t, quarter, wide), small),
            DMA((4,)),
            DMA((n_f, SPLIT)),
            DMA((n_b, n_t)),
            DMA((n_b, n_t)),
            DMA((n_b,)),
            DMA((n_b,)),
            DMA((n_b, n_z)),
            DMA((n_b, n_z)),
            DMA((n_b, n_z)),
            DMA((n_b, n_z)),
            DMA((n_b, share)),
            DMA((n_b, share)),
            DMA((n_b, n_z, 3)),
            DMA((n_b, n_f)),
            DMA((n_b, 3)),
            DMA((n_b, 3)),
            DMA((n_b,)),
            DMA((n_f, SPLIT)),
            DMA((SPLIT, n_t - 1)),
            DMA((SPLIT, n_t - 1)),
        ],
        compiler_params=pltpu.CompilerParams(
            collective_id=0, has_side_effects=True, vmem_limit_bytes=67043328
        ),
        name="layer",
    )(inverse, pieces, pair, w_query, w_key, w_value, w_out, fac, faco)


def stationary_body(
    n_f, n_t, hidden, w_query, w_key, w_value, w_out, exp_query, exp_key, exp_value, exp_out, owner
):
    slab = w_query.shape[0]
    block = hidden.shape[1] // exp_query.shape[0]
    q_cols, k_cols = w_query.shape[1], w_key.shape[1]
    pieces, pair, fac, faco, inverse = arrange(
        n_f, n_t, block, owner, hidden, (exp_query, exp_key, exp_value, exp_out),
        q_cols + 2 * k_cols, w_out.shape[0], slab,
    )
    return layer(
        n_f, n_t, q_cols // k_cols, block, inverse, pieces, pair, w_query, w_key, w_value, w_out,
        fac, faco,
    )


def solution(mesh):
    n_f, n_t = mesh.shape["fsdp"], mesh.shape["tp"]

    def body(*arrays):
        hidden, w_query, w_key = arrays[0], arrays[1], arrays[2]
        heads, kv_heads = w_query.shape[1] // HD, w_key.shape[1] // HD
        share = heads // kv_heads
        fits = (
            heads == n_f
            and n_t == SIDE * SIDE
            and n_f % n_t == 0
            and n_f == LINE * CORES
            and hidden.shape[0] % (16 * SPLIT * n_t) == 0
            and hidden.shape[0] % (16 * SPLIT * share) == 0
        )
        if fits:
            return stationary_body(n_f, n_t, *arrays)
        return gather_body(*arrays)

    placed = (
        P("fsdp", None),
        P("fsdp", "tp"),
        P("fsdp", "tp"),
        P("fsdp", "tp"),
        P("tp", "fsdp"),
        P(),
        P(),
        P(),
        P(),
        P(),
    )
    return jax.shard_map(
        body, mesh=mesh, in_specs=placed, out_specs=P("fsdp", "tp"), check_vma=False
    )
```

time: 264 us -> 242 us (0.917)
  the two profiles are of different devices: /device:TPU:17 before, /device:TPU:25 now
where the time goes in v3:
time: 242 us; the launch traced here: 241 us
  Pallas kernels  234 us (97%)
  local copies, waits for them, and re-layouts  6.66 us (3%)
    pallas_call x1, Pallas kernels, layer(): pl.pallas_call(partial(layer_kernel, n_f, n_t, share, block), out_shape=j...  230 us
    unnamed x4, local copies, waits for them, and re-layouts  6.66 us

profile of v3, /device:TPU:25, one launch (start us, length us, event | category | flops | bytes accessed | tf_op | source)
XLA Modules:
  0.0 241.1 jit_solution(2425988556196967045)
XLA Ops:
  0.0 1.4 copy.11.eq_hbm
  1.4 1.4 copy.12.ek_hbm
  2.8 1.4 copy.13.ev_hbm
  4.2 4.2 %arrange.1 = (bf16[8,2,48,896]{3,2,1,0:T(8,128)(2,1)}, bf16[2,384,896]{2,1,0:T(8,128)(2,1)}, f32[8,1536]{1,0:T(8,128)}, f32[8,896]{1,0:T(8,128)}, s32[8]{0:T(128)}) custom-call(s32[8]{0:T(128)} %owner_ref.1, s32[56,32]{1,0:T(8,128)} %copy.11.eq_hbm, s32[56,8]{1,0:T(8,128)} %copy.12.ek_hbm, s32[56,8]{1,0:T(8,128)} %copy.13.ev_hbm, s32[32,56]{1,0:T(8,128)} %eo_hbm.1, ...), custom_call_target="tpu_custom_call" | custom-call | tf_op jit(solution)/shard_map/arrange/pallas_call | solution.py:266
  8.4 230.3 %layer.1 = bf16[384,1792]{1,0:T(8,128)(2,1)} custom-call(s32[8]{0:T(128)} %get-tuple-element.10.inverse_ref, bf16[8,2,48,896]{3,2,1,0:T(8,128)(2,1)} %get-tuple-element.11.pieces, bf16[2,384,896]{2,1,0:T(8,128)(2,1)} %get-tuple-element.12.pair_ref, bf16[896,1024]{1,0:T(8,128)(2,1)} %wq_ref.1, bf16[896,256]{1,0:T(8,128)(2,1)} %wk_ref.1, ...), custom_call_target="tpu_custom_call" | custom-call | tf_op jit(solution)/shard_map/layer/pallas_call | solution.py:794
  238.6 2.5 %copy.15 = bf16[384,1792]{1,0:T(8,128)(2,1)} copy(bf16[384,1792]{1,0:T(8,128)(2,1)} %layer.1) | data formatting | bytes 2752512

commit v4 on v3

--- a/solution.py
+++ b/solution.py
@@ -232,12 +232,12 @@
     logical = owner_ref[f]
     blocks = slab // block
 
-    def spread_out(exponents, first, width):
-        shape = (exponents.shape[1], width)
+    def spread_out(powers, first, width):
+        shape = (powers.shape[1], width)
         block_of = lax.broadcasted_iota(jnp.int32, shape, 1) // block + first
         chosen = lax.broadcasted_iota(jnp.int32, shape, 0) == block_of
         return jnp.dot(
-            jnp.exp2(exponents.astype(jnp.float32)),
+            powers,
             chosen.astype(jnp.float32),
             preferred_element_type=jnp.float32,
         )
@@ -246,11 +246,20 @@
         copy.wait()
     at = 0
     for ref in (eq_ref, ek_ref, ev_ref):
-        cols = ref.shape[1] // n_t
-        picked = ref[pl.ds(logical * blocks, blocks), :]
-        in_ref[:blocks, at : at + cols * block] = spread_out(picked, t * cols, cols * block)
+        cols = ref.shape[0] // n_t
+        shape = (in_ref.shape[0], ref.shape[1])
+        row_of = lax.broadcasted_iota(jnp.int32, shape, 0) + logical * blocks
+        chosen = lax.broadcasted_iota(jnp.int32, shape, 1) == row_of
+        picked = lax.dot_general(
+            chosen.astype(jnp.float32),
+            jnp.exp2(ref[...].astype(jnp.float32)),
+            (((1,), (1,)), ((), ())),
+            preferred_element_type=jnp.float32,
+        )
+        in_ref[:, at : at + cols * block] = spread_out(picked, t * cols, cols * block)
         at += cols * block
     picked = eo_ref[span_at(t, eo_ref.shape[0] // n_t), :]
+    picked = jnp.exp2(picked.astype(jnp.float32))
     out_ref[: picked.shape[0], :] = spread_out(picked, logical * blocks, slab)
     for i in range(n_f):
         inverse_ref[owner_ref[i]] = i
@@ -325,7 +334,7 @@
     return (accum / row_sum).astype(jnp.bfloat16)
 
 
-SPAN = 2
+SPAN = 4
 PROJECT = 2
 PAIR = PROJECT + 1
 CLOSE = PAIR + LINE - 1
@@ -633,9 +642,6 @@
         def _():
             close(s - CLOSE)
 
-        for d in range(1, n_z):
-            relay(s, d)
-
         @pl.when(within(s - ATTEND, n_b))
         def _():
             i = s - ATTEND
@@ -652,6 +658,9 @@
                 line_copy(i, z, below, 2).start()
 
             line_copy(i, z, partner, 0).start()
+
+        for d in range(1, n_z):
+            relay(s, d)
 
         @pl.when(within(s - ATTEND - n_z, n_b))
         def _():
@@ -850,7 +859,7 @@
     block = hidden.shape[1] // exp_query.shape[0]
     q_cols, k_cols = w_query.shape[1], w_key.shape[1]
     pieces, pair, fac, faco, inverse = arrange(
-        n_f, n_t, block, owner, hidden, (exp_query, exp_key, exp_value, exp_out),
+        n_f, n_t, block, owner, hidden, (exp_query.T, exp_key.T, exp_value.T, exp_out),
         q_cols + 2 * k_cols, w_out.shape[0], slab,
     )
     return layer(

time: 242 us -> 235 us (0.971)
  local copies, waits for them, and re-layouts: 6.66 us -> 2.51 us
  Pallas kernels: 234 us -> 231 us
    unnamed x4 -> x1, local copies, waits for them, and re-layouts: 6.66 us -> 2.51 us
    pallas_call x1, Pallas kernels: 230 us -> 227 us  [layer(): pl.pallas_call(partial(layer_kernel, n_f, n_t, share, block), out_shape=j...]
where the time goes in v4:
time: 235 us; the launch traced here: 234 us
  Pallas kernels  231 us (98%)
  local copies, waits for them, and re-layouts  2.51 us (1%)
    pallas_call x1, Pallas kernels, layer(): pl.pallas_call(partial(layer_kernel, n_f, n_t, share, block), out_shape=j...  227 us

profile of v4, /device:TPU:25, one launch (start us, length us, event | category | flops | bytes accessed | tf_op | source)
XLA Modules:
  0.0 233.9 jit_solution(2025790707270181673)
XLA Ops:
  0.0 4.4 %arrange.1 = (bf16[8,2,48,896]{3,2,1,0:T(8,128)(2,1)}, bf16[2,384,896]{2,1,0:T(8,128)(2,1)}, f32[8,1536]{1,0:T(8,128)}, f32[8,896]{1,0:T(8,128)}, s32[8]{0:T(128)}) custom-call(s32[8]{0:T(128)} %owner_ref.1, s32[32,56]{1,0:T(8,128)} %bitcast.3, s32[8,56]{1,0:T(8,128)} %bitcast.4, s32[8,56]{1,0:T(8,128)} %bitcast.5, s32[32,56]{1,0:T(8,128)} %eo_hbm.1, ...), custom_call_target="tpu_custom_call" | custom-call | tf_op jit(solution)/shard_map/arrange/pallas_call | solution.py:275
  4.4 226.9 %layer.1 = bf16[384,1792]{1,0:T(8,128)(2,1)} custom-call(s32[8]{0:T(128)} %get-tuple-element.10.inverse_ref, bf16[8,2,48,896]{3,2,1,0:T(8,128)(2,1)} %get-tuple-element.11.pieces, bf16[2,384,896]{2,1,0:T(8,128)(2,1)} %get-tuple-element.12.pair_ref, bf16[896,1024]{1,0:T(8,128)(2,1)} %wq_ref.1, bf16[896,256]{1,0:T(8,128)(2,1)} %wk_ref.1, ...), custom_call_target="tpu_custom_call" | custom-call | tf_op jit(solution)/shard_map/layer/pallas_call | solution.py:803
  231.4 2.5 %copy.12 = bf16[384,1792]{1,0:T(8,128)(2,1)} copy(bf16[384,1792]{1,0:T(8,128)(2,1)} %layer.1) | data formatting | bytes 2752512

commit v5 on v4

--- a/solution.py
+++ b/solution.py
@@ -429,14 +429,10 @@
             {"fsdp": partner},
         ).wait_recv()
 
-    def either(i):
-        first = lax.rem(i, 2)
-        return along[0] + first * (along[1] - along[0]), along[1] + first * (along[0] - along[1])
-
     def diagonal_copy(i):
         return remote(
             y.at[i, across], half_in.at[i], sum_send.at[i, 2], sum_recv.at[i, 2],
-            {"tp": either(i)[0]},
+            {"tp": across},
         )
 
     def full_copy(i, k):
@@ -674,22 +670,14 @@
             for r in range(n_t):
                 y[i, r] = part[r * quarter : (r + 1) * quarter, :slab]
             diagonal_copy(i).start()
+            for k in range(2):
+                full_copy(i, k).start()
 
         @pl.when(within(s - ATTEND - n_z - 1, n_b))
         def _():
             i = s - ATTEND - n_z - 1
             diagonal_copy(i).wait_recv()
-            to = either(i)[1]
-            y[i, to] = (y[i, to].astype(jnp.float32) + half_in[i].astype(jnp.float32)).astype(
-                jnp.bfloat16
-            )
-            for k in range(2):
-                full_copy(i, k).start()
-
-        @pl.when(within(s - ATTEND - n_z - 2, n_b))
-        def _():
-            i = s - ATTEND - n_z - 2
-            summed = y[i, t].astype(jnp.float32)
+            summed = y[i, t].astype(jnp.float32) + half_in[i].astype(jnp.float32)
             for k in range(2):
                 full_copy(i, k).wait_recv()
                 summed = summed + full_in[i, k].astype(jnp.float32)
@@ -707,7 +695,7 @@
 
         for p in range(SPLIT):
 
-            @pl.when(s - ATTEND - n_z - 3 == f * SPLIT + p)
+            @pl.when(s - ATTEND - n_z - 2 == f * SPLIT + p)
             def _():
                 for d in range(1, n_f):
                     source = lax.rem(f + d, n_f)
@@ -724,7 +712,7 @@
 
         return carry
 
-    lax.fori_loop(0, n_b + ATTEND + n_z + 3, step, 0)
+    lax.fori_loop(0, n_b + ATTEND + n_z + 2, step, 0)
 
     def finish_head(b, carry):
         for k in range(1, share):

time: 235 us -> 234 us (level)
  no operation moved by 1% of the time
where the time goes in v5:
time: 234 us
  Pallas kernels  232 us (99%)
  local copies, waits for them, and re-layouts  2.51 us (1%)
    pallas_call x1, Pallas kernels, layer(): pl.pallas_call(partial(layer_kernel, n_f, n_t, share, block), out_shape=j...  227 us

profile of v5, /device:TPU:25, one launch (start us, length us, event | category | flops | bytes accessed | tf_op | source)
XLA Modules:
  0.0 234.4 jit_solution(1290560535066026589)
XLA Ops:
  0.0 4.4 %arrange.1 = (bf16[8,2,48,896]{3,2,1,0:T(8,128)(2,1)}, bf16[2,384,896]{2,1,0:T(8,128)(2,1)}, f32[8,1536]{1,0:T(8,128)}, f32[8,896]{1,0:T(8,128)}, s32[8]{0:T(128)}) custom-call(s32[8]{0:T(128)} %owner_ref.1, s32[32,56]{1,0:T(8,128)} %bitcast.3, s32[8,56]{1,0:T(8,128)} %bitcast.4, s32[8,56]{1,0:T(8,128)} %bitcast.5, s32[32,56]{1,0:T(8,128)} %eo_hbm.1, ...), custom_call_target="tpu_custom_call" | custom-call | tf_op jit(solution)/shard_map/arrange/pallas_call | solution.py:275
  4.4 227.5 %layer.1 = bf16[384,1792]{1,0:T(8,128)(2,1)} custom-call(s32[8]{0:T(128)} %get-tuple-element.10.inverse_ref, bf16[8,2,48,896]{3,2,1,0:T(8,128)(2,1)} %get-tuple-element.11.pieces, bf16[2,384,896]{2,1,0:T(8,128)(2,1)} %get-tuple-element.12.pair_ref, bf16[896,1024]{1,0:T(8,128)(2,1)} %wq_ref.1, bf16[896,256]{1,0:T(8,128)(2,1)} %wk_ref.1, ...), custom_call_target="tpu_custom_call" | custom-call | tf_op jit(solution)/shard_map/layer/pallas_call | solution.py:791
  231.9 2.5 %copy.12 = bf16[384,1792]{1,0:T(8,128)(2,1)} copy(bf16[384,1792]{1,0:T(8,128)(2,1)} %layer.1) | data formatting | bytes 2752512
